TPU v7x, 32 devices: a whole 2x2x4 slice. The times are simulated.
32 devices in a mesh: blk: 32 (over z, y, x, core).
Axes of the slice: x: 2, y: 2, z: 4, core: 2. Of those that a mesh axis runs over, the one named last changes fastest.
Arguments:
- image_features: bfloat16 [8192, 1536], P('blk'), may hold values from -0.119628906 to 0.119628906
- head_weight: bfloat16 [1536, 1152], P('blk'), may hold values from -0.15625 to 0.15625
- text_embeds: bfloat16 [8192, 1152], P('blk'), may hold values from -0.29882812 to 0.29882812
- natural_exponent_factor: float32 [1], replicated, may hold values from 1.6 to 2.6
- logit_bias: float32 [1], replicated, may hold values from -4 to -1
Outputs:
- grad_features: bfloat16 [8192, 1536], P('blk')
- grad_text: bfloat16 [8192, 1152], P('blk')
- grad_weight: float32 [1536, 1152], P('blk')
All inputs are finite; a program needn't handle non-finite values.
Results may differ from a plain program's by a relative error of at most 0.0085.
Values may be sent and summed in bfloat16 or wider, within the bound.
A program may use at most 64 MiB of HBM per device.

v0:
```python
import functools

import jax
import jax.numpy as jnp
from jax import lax
from jax.experimental import pallas as pl
from jax.experimental.pallas import tpu as pltpu
from jax.sharding import PartitionSpec as P

S = 4
epsilon = 1e-06
MESH = pl.DeviceIdType.MESH
F32 = jnp.float32
BF = jnp.bfloat16


def dot_nt(a, b):
    return lax.dot_general(a, b, (((1,), (1,)), ((), ())), preferred_element_type=F32)


def pair_grad(rows, cols, t, bias, own):
    logits = t * dot_nt(rows, cols) + bias
    if own:
        matched = lax.broadcasted_iota(jnp.int32, logits.shape, 0) == lax.broadcasted_iota(
            jnp.int32, logits.shape, 1
        )
        z = jnp.where(matched, 1.0, -1.0).astype(F32)
        return (-t * z * jax.nn.sigmoid(-z * logits)).astype(BF)
    return (t * jax.nn.sigmoid(logits)).astype(BF)


def sem_keys(depth):
    keys = ["za", "zb", "g3a", "g3b"] + [("z", d) for d in range(1, depth)]
    for d in range(depth):
        keys += [("x1", d), ("y1", d), ("y3", d, 0), ("y3", d, 1), ("x3", d, 0), ("x3", d, 1)]
        keys += [("w", d, i) for i in range(8)]
        keys += [(k, d) for k in ("g0", "g1a", "g1b", "g2a", "g2b")]
    for k in ("t", "i"):
        keys += [(k, "in", 0), (k, "in", 1), (k, "on", 0), (k, "on", 1), (k, "far", 0), (k, "far", 1)]
        keys += [(k, "relay", 0), (k, "relay", 1)]
    return {k: i for i, k in enumerate(keys)}


def kernel(
    n, axis, keys,
    x_ref, w_ref, t_ref, lf_ref, bias_ref,
    gx_ref, gt_ref, gw_ref,
    w_all, text_low, text_in, image_low, image_in, xt, gz, from_core, to_core,
    s1a, s1b, r1a, r1b, s2a, s2b, r2a, r2b, s3a, s3b, r3a, r3b,
    send_sem, recv_sem,
):
    depth = n // 8
    opp = depth // 2
    near = [d for d in range(1, depth) if d != opp]
    rows, width = x_ref.shape
    own_rows, cols = w_ref.shape
    half = rows // 2
    ha = (cols // 128 + 1) // 2 * 128
    A, B = pl.ds(0, ha), pl.ds(ha, cols - ha)
    me = lax.axis_index(axis)
    core = lax.rem(me, 2)
    chip = me // 2
    x = lax.rem(chip, 2)
    y = lax.rem(chip // 2, 2)
    z = chip // 4

    def dev(z_, y_, x_, c_):
        return ((z_ * 2 + y_) * 2 + x_) * 2 + c_

    def up(d):
        return lax.rem(z + d, depth)

    def down(d):
        return lax.rem(z + depth - d, depth)

    xn, yn, partner = dev(z, y, 1 - x, core), dev(z, 1 - y, x, core), dev(z, y, x, 1 - core)
    sent = []
    sent_if = []

    def copy(src, dst, key, target):
        i = keys[key]
        return pltpu.make_async_remote_copy(
            src_ref=src, dst_ref=dst, send_sem=send_sem.at[i], recv_sem=recv_sem.at[i],
            device_id=(target,), device_id_type=MESH,
        )

    def send(src, dst, key, target):
        c = copy(src, dst, key, target)
        c.start()
        sent.append(c)

    def arrived(dst, key):
        copy(dst, dst, key, partner).wait_recv()

    barrier = pltpu.get_barrier_semaphore()
    first = me - core
    peers = [partner, xn, yn] + [dev(up(d), y, x, core) for d in range(1, depth)]
    peers += [lax.rem(first + n - 2 + c, n) for c in range(2)]
    peers += [lax.rem(first + 2 + c, n) for c in range(2)]
    peers += [lax.rem(me + n - 3 + 6 * core, n)]
    for peer in peers:
        pl.semaphore_signal(barrier, inc=1, device_id=(peer,), device_id_type=MESH)

    t = jnp.exp(jnp.full((1, 1), lf_ref[0], F32))
    bias = bias_ref[0]
    text = t_ref[...].astype(F32)
    text_length = jnp.sqrt(jnp.sum(text * text, axis=1, keepdims=True) + epsilon)
    text_low[...] = (text / text_length).astype(BF)
    w_all[me] = w_ref[...]

    pl.semaphore_wait(barrier, len(peers))

    send(w_ref.at[:, A], w_all.at[me, :, A], ("x1", 0), xn)
    send(w_ref.at[:, B], w_all.at[me, :, B], ("y1", 0), yn)
    for d in near:
        send(w_ref, w_all.at[me], ("z", d), dev(up(d), y, x, core))
    send(w_ref.at[:, A], w_all.at[me, :, A], ("y3", 0, 0), yn)
    send(w_ref.at[:, B], w_all.at[me, :, B], ("x3", 0, 0), xn)
    send(w_ref, w_all.at[me], ("w", 0, 0), partner)

    below, above = lax.rem(me + n - 2, n), lax.rem(me + 2, n)

    def halves(buf, slots, q, key, kind, base, cond, far=False):
        for c in range(2):
            part = pl.ds(c * half, half)
            cp = pltpu.make_async_remote_copy(
                src_ref=buf.at[part], dst_ref=slots.at[q, part],
                send_sem=send_sem.at[keys[(key, kind, c)]],
                recv_sem=recv_sem.at[keys[(key, "in", 0)] + q],
                device_id=(base + c,), device_id_type=MESH,
            )
            if far:
                arrived(slots.at[2, part], (key, "far", c))
            pl.when(cond)(cp.start)
            sent_if.append((cond, cp))

    def send_far(buf, slots, key, far):
        for c in range(2):
            part = pl.ds(c * half, half)
            send(buf.at[part], slots.at[2, part], (key, "far", c), far)

    def relay_far(slots, key, q, cond):
        halves(slots.at[2], slots, q, key, "relay", xn - core, cond, True)

    def swap_block(slots, key):
        part = pl.ds(pl.multiple_of(core * half, half), half)
        for q in range(2):
            arrived(slots.at[q, part], (key, "in", q))
            send(slots.at[q, part], slots.at[q, part], (key, "on", q), partner)

    def wait_block(slots, key, q):
        part = pl.ds(pl.multiple_of((1 - core) * half, half), half)
        arrived(slots.at[q, part], (key, "on", q))


    def onward(part, d, key_a, key_b):
        if key_a is not None and d == opp - 1:
            send(part(A), part(A), key_a, dev(up(1), y, x, core))
        if key_b is not None and d == opp + 1:
            send(part(B), part(B), key_b, dev(down(1), y, x, core))

    def step_z(d):
        s = dev(down(d), y, x, core)

        def part(cut):
            return w_all.at[s, :, cut]

        if d == opp:
            arrived(part(A), "za")
            send(part(A), part(A), ("y3", d, 0), yn)
            send(part(A), part(A), ("w", d, 0), partner)
            arrived(part(B), "zb")
            send(part(B), part(B), ("x3", d, 0), xn)
            send(part(B), part(B), ("w", d, 7), partner)
            return
        arrived(w_all.at[s], ("z", d))
        onward(part, d, "za", "zb")
        send(part(A), part(A), ("y3", d, 0), yn)
        send(part(B), part(B), ("x3", d, 0), xn)
        send(w_all.at[s], w_all.at[s], ("w", d, 0), partner)

    def step_one(d):
        def side(cut):
            return w_all.at[dev(down(d), y, 1 - x, core), :, cut]

        def front(cut):
            return w_all.at[dev(down(d), 1 - y, x, core), :, cut]

        s = side(A)
        arrived(s, ("x1", d))
        if d == 0:
            for e in near:
                send(s, s, ("x1", e), dev(up(e), y, x, core))
        onward(side, d, ("x1", opp), None)
        send(s, s, ("y3", d, 1), yn)
        send(s, s, ("w", d, 1), partner)
        s = front(B)
        arrived(s, ("y1", d))
        if d == 0:
            for e in near:
                send(s, s, ("y1", e), dev(up(e), y, x, core))
        onward(front, d, None, ("y1", opp))
        send(s, s, ("x3", d, 1), xn)
        send(s, s, ("w", d, 2), partner)

    def step_two(d):
        for i, x_ in enumerate((x, 1 - x)):
            s = w_all.at[dev(down(d), 1 - y, x_, core), :, A]
            arrived(s, ("y3", d, i))
            send(s, s, ("w", d, 3 + i), partner)
        for i, y_ in enumerate((y, 1 - y)):
            s = w_all.at[dev(down(d), y_, 1 - x, core), :, B]
            arrived(s, ("x3", d, i))
            send(s, s, ("w", d, 5 + i), partner)

    send_far(text_low, text_in, "t", lax.rem(me + n - 3 + 2 * core, n))
    step_one(0)
    for d in near:
        step_z(d)
    passed_on = jnp.logical_and(x == 0, core == 0)
    halves(text_low, text_in, core, "t", "in", below - core, jnp.logical_not(passed_on))
    for d in near:
        step_one(d)
    relay_far(text_in, "t", 0, jnp.logical_and(x == 0, core == 1))
    step_z(opp)
    step_one(opp)
    for d in [0] + near + [opp]:
        step_two(d)

    xt[...] = x_ref[...].T

    other = 1 - core
    for d in range(depth):
        zs = down(d)
        if d == opp:
            arrived(w_all.at[dev(zs, y, x, other), :, A], ("w", d, 0))
            arrived(w_all.at[dev(zs, y, x, other), :, B], ("w", d, 7))
        else:
            arrived(w_all.at[dev(zs, y, x, other)], ("w", d, 0))
        arrived(w_all.at[dev(zs, y, 1 - x, other), :, A], ("w", d, 1))
        arrived(w_all.at[dev(zs, 1 - y, x, other), :, B], ("w", d, 2))
        for i, x_ in enumerate((x, 1 - x)):
            arrived(w_all.at[dev(zs, 1 - y, x_, other), :, A], ("w", d, 3 + i))
        for i, y_ in enumerate((y, 1 - y)):
            arrived(w_all.at[dev(zs, y_, 1 - x, other), :, B], ("w", d, 5 + i))

    weight = w_all[...].reshape(n * own_rows, cols)
    embedded = jnp.dot(x_ref[...], weight, preferred_element_type=F32)
    image_length = jnp.sqrt(jnp.sum(embedded * embedded, axis=1, keepdims=True) + epsilon)
    image_unit = embedded / image_length
    image_low[...] = image_unit.astype(BF)
    mine = image_low[...]
    own_text = text_low[...]

    grad = pair_grad(mine, own_text, t, bias, True)
    image_grad = jnp.dot(grad, own_text, preferred_element_type=F32)
    send_far(image_low, image_in, "i", lax.rem(me + 1 + 2 * core, n))
    passed_on = jnp.logical_and(x == 1, core == 1)
    halves(image_low, image_in, core, "i", "in", above - core, jnp.logical_not(passed_on))

    swap_block(text_in, "t")
    for q in (2, 0, 1):
        if q < 2:
            wait_block(text_in, "t", q)
        block = text_in[q]
        image_grad += jnp.dot(
            pair_grad(mine, block, t, bias, False), block, preferred_element_type=F32
        )
    along = jnp.sum(image_unit * image_grad, axis=1, keepdims=True)
    embed_grad = ((image_grad - image_unit * along) / image_length).astype(BF)

    order = [opp] + near + [0]
    group = 8 * own_rows
    for d in order:
        lhs = xt[pl.ds(pl.multiple_of(up(d) * group, group), group), :]
        part = jnp.dot(lhs, embed_grad, preferred_element_type=F32)
        gz[d] = part.reshape(4, 2, own_rows, cols)
        for c in range(4):
            to_core[d, c] = gz[d, c, other].astype(BF)
        send(to_core.at[d], from_core.at[d], ("g0", d), partner)

    def base(d, c, cut):
        return gz[d, c, core, :, cut] + from_core[d, c, :, cut].astype(F32)

    relay_far(image_in, "i", 1, jnp.logical_and(x == 1, core == 0))
    gx_ref[...] = dot_nt(embed_grad, weight).astype(BF)

    for d in order:
        arrived(from_core.at[d], ("g0", d))
        for i in range(2):
            s1a[d, i] = base(d, (1 - y) * 2 + i, A).astype(BF)
            s1b[d, i] = base(d, i * 2 + 1 - x, B).astype(BF)
        send(s1a.at[d], r1a.at[d], ("g1a", d), yn)
        send(s1b.at[d], r1b.at[d], ("g1b", d), xn)

    text_grad = jnp.dot(
        pair_grad(own_text, mine, t, bias, True), mine, preferred_element_type=F32
    )

    def stage_two(d):
        arrived(r1a.at[d], ("g1a", d))
        arrived(r1b.at[d], ("g1b", d))
        if d == opp - 1:
            arrived(r2a.at[opp], ("g2a", opp))
        if d == opp + 1:
            arrived(r2b.at[opp], ("g2b", opp))
        for i in range(2):
            left = base(d, y * 2 + i, A) + r1a[d, i].astype(F32)
            right = base(d, i * 2 + x, B) + r1b[d, i].astype(F32)
            if d == opp - 1:
                left += r2a[opp, i].astype(F32)
            if d == opp + 1:
                right += r2b[opp, i].astype(F32)
            s2a[d, i] = left.astype(BF)
            s2b[d, i] = right.astype(BF)
        ta, tb = (up(1), down(1)) if d == opp else (up(d), up(d))
        send(s2a.at[d], r2a.at[d], ("g2a", d), dev(ta, y, x, core))
        send(s2b.at[d], r2b.at[d], ("g2b", d), dev(tb, y, x, core))

    def gathered(i, j):
        left = base(0, y * 2 + i, A) + r1a[0, i].astype(F32)
        right = base(0, j * 2 + x, B) + r1b[0, j].astype(F32)
        for d in near:
            left += r2a[d, i].astype(F32)
            right += r2b[d, j].astype(F32)
        return left, right

    swap_block(image_in, "i")
    for d in [opp] + near:
        stage_two(d)

    for q in (2, 0, 1):
        if q < 2:
            wait_block(image_in, "i", q)
        block = image_in[q]
        text_grad += jnp.dot(
            pair_grad(own_text, block, t, bias, False), block, preferred_element_type=F32
        )
    arrived(r1a.at[0], ("g1a", 0))
    arrived(r1b.at[0], ("g1b", 0))
    for d in near:
        arrived(r2a.at[d], ("g2a", d))
        arrived(r2b.at[d], ("g2b", d))
    left, right = gathered(1 - x, 1 - y)
    s3a[...] = left.astype(BF)
    s3b[...] = right.astype(BF)
    send(s3a, r3a, "g3a", xn)
    send(s3b, r3b, "g3b", yn)
    left, right = gathered(x, y)
    gw_ref[:, A] = left
    gw_ref[:, B] = right
    text_unit = t_ref[...].astype(F32) / text_length
    along = jnp.sum(text_unit * text_grad, axis=1, keepdims=True)
    gt_ref[...] = ((text_grad - text_unit * along) / text_length).astype(BF)

    arrived(r3a, "g3a")
    arrived(r3b, "g3b")
    gw_ref[:, A] += r3a[...].astype(F32)
    gw_ref[:, B] += r3b[...].astype(F32)
    for c in sent:
        c.wait_send()
    for cond, c in sent_if:
        pl.when(cond)(c.wait_send)


def fused(n, axis, image_features, head_weight, text_embeds, factor, bias):
    depth = n // 8
    rows, width = image_features.shape
    own_rows, cols = head_weight.shape
    keys = sem_keys(depth)
    ha = (cols // 128 + 1) // 2 * 128
    hb = cols - ha
    vmem = pl.BlockSpec(memory_space=pltpu.VMEM)
    smem = pl.BlockSpec(memory_space=pltpu.SMEM)
    scratch = [
        ((n, own_rows, cols), BF),
        ((rows, cols), BF),
        ((3, rows, cols), BF),
        ((rows, cols), BF),
        ((3, rows, cols), BF),
        ((width, rows), BF),
        ((depth, 4, 2, own_rows, cols), F32),
        ((depth, 4, own_rows, cols), BF),
        ((depth, 4, own_rows, cols), BF),
        ((depth, 2, own_rows, ha), BF),
        ((depth, 2, own_rows, hb), BF),
        ((depth, 2, own_rows, ha), BF),
        ((depth, 2, own_rows, hb), BF),
        ((depth, 2, own_rows, ha), BF),
        ((depth, 2, own_rows, hb), BF),
        ((depth, 2, own_rows, ha), BF),
        ((depth, 2, own_rows, hb), BF),
        ((own_rows, ha), BF),
        ((own_rows, hb), BF),
        ((own_rows, ha), BF),
        ((own_rows, hb), BF),
    ]
    return pl.pallas_call(
        functools.partial(kernel, n, axis, keys),
        out_shape=(
            jax.ShapeDtypeStruct((rows, width), BF),
            jax.ShapeDtypeStruct((rows, cols), BF),
            jax.ShapeDtypeStruct((own_rows, cols), F32),
        ),
        in_specs=[vmem, vmem, vmem, smem, smem],
        out_specs=(vmem, vmem, vmem),
        scratch_shapes=[pltpu.VMEM(s, d) for s, d in scratch]
        + [pltpu.SemaphoreType.DMA((len(keys),))] * 2,
        compiler_params=pltpu.CompilerParams(
            collective_id=0, has_side_effects=True, vmem_limit_bytes=60 * 2**20
        ),
    )(image_features, head_weight, text_embeds, factor, bias)


def passed_along(block, axis, distance):
    devices = range(lax.axis_size(axis))
    route = [((i - distance) % len(devices), i) for i in devices]
    return lax.ppermute(block, axis, route)


def normalize(rows):
    squares = jnp.sum(rows * rows, axis=1, keepdims=True)
    length = jnp.sqrt(squares + epsilon)
    return (rows / length, length)


def similarity_derivative(
    picture_sample_group,
    caption_sample_group,
    similarity_multiplier,
    neighbour_distance,
    outer_dimension_size,
):
    similarity_matrix = (
        similarity_multiplier
        * lax.dot_general(
            picture_sample_group,
            caption_sample_group,
            (((1,), (1,)), ((), ())),
            preferred_element_type=jnp.float32,
        )
        + neighbour_distance
    )
    if outer_dimension_size:
        matched = lax.broadcasted_iota(
            jnp.int32, similarity_matrix.shape, 0
        ) == lax.broadcasted_iota(jnp.int32, similarity_matrix.shape, 1)
        match_polarity = jnp.where(matched, 1.0, -1.0).astype(jnp.float32)
    else:
        match_polarity = -jnp.ones(similarity_matrix.shape, jnp.float32)
    return (
        -similarity_multiplier
        * match_polarity
        * jax.nn.sigmoid(-match_polarity * similarity_matrix)
    ).astype(jnp.bfloat16)


def project_back(grad, unit_rows, length):
    return (grad - unit_rows * jnp.sum(unit_rows * grad, axis=1, keepdims=True)) / length


def by_collectives(image_features, head_weight, text_embeds, natural_exponent_factor, logit_bias):
    full_weight = lax.all_gather(head_weight, "blk", axis=0, tiled=True)
    embedded = jnp.dot(image_features, full_weight, preferred_element_type=jnp.float32)
    image_unit, image_length = normalize(embedded)
    picture_embedding_mapped = image_unit.astype(jnp.bfloat16)
    text_unit, text_length = normalize(text_embeds.astype(jnp.float32))
    text_low = text_unit.astype(jnp.bfloat16)
    similarity_multiplier = jnp.exp(natural_exponent_factor[0])
    neighbour_distance = logit_bias[0]
    image_grad = jnp.zeros(image_unit.shape, jnp.float32)
    current_neighbour_tile = text_low
    for partition_portion in range(S):
        mapping_matrix = similarity_derivative(
            picture_embedding_mapped,
            current_neighbour_tile,
            similarity_multiplier,
            neighbour_distance,
            partition_portion == 0,
        )
        image_grad = image_grad + jnp.dot(
            mapping_matrix, current_neighbour_tile, preferred_element_type=jnp.float32
        )
        if partition_portion + 1 < S:
            current_neighbour_tile = passed_along(current_neighbour_tile, "blk", -1)
    text_grad = jnp.zeros(text_unit.shape, jnp.float32)
    passing = picture_embedding_mapped
    for partition_portion in range(S):
        mapping_matrix = similarity_derivative(
            passing, text_low, similarity_multiplier, neighbour_distance, partition_portion == 0
        )
        text_grad = text_grad + lax.dot_general(
            mapping_matrix, passing, (((0,), (0,)), ((), ())), preferred_element_type=jnp.float32
        )
        if partition_portion + 1 < S:
            passing = passed_along(passing, "blk", 1)
    embed_grad = project_back(image_grad, image_unit, image_length).astype(jnp.bfloat16)
    grad_text = project_back(text_grad, text_unit, text_length).astype(jnp.bfloat16)
    grad_features = lax.dot_general(
        embed_grad, full_weight, (((1,), (1,)), ((), ())), preferred_element_type=jnp.float32
    ).astype(jnp.bfloat16)
    grad_weight = lax.psum_scatter(
        lax.dot_general(
            image_features, embed_grad, (((0,), (0,)), ((), ())), preferred_element_type=jnp.float32
        ),
        "blk",
        scatter_dimension=0,
        tiled=True,
    )
    return (grad_features, grad_text, grad_weight)


def on_device(image_features, head_weight, text_embeds, natural_exponent_factor, logit_bias):
    n = lax.axis_size("blk")
    whole_tiles = head_weight.shape[0] % 16 == 0 and n % 16 == 0 and n > 16
    run = functools.partial(fused, n, "blk") if whole_tiles else by_collectives
    return run(image_features, head_weight, text_embeds, natural_exponent_factor, logit_bias)


def solution(mesh):
    return jax.shard_map(
        on_device,
        mesh=mesh,
        in_specs=(P("blk", None), P("blk", None), P("blk", None), P(), P()),
        out_specs=(P("blk", None), P("blk", None), P("blk", None)),
        check_vma=False,
    )
```

profile of v0, /device:TPU:0, one launch (start us, length us, event | category | flops | bytes accessed | tf_op | source)
XLA Modules:
  0.0 88.8 jit_solution(16618870980561034328)
XLA Ops:
  1.9 82.9 %shard_map.76 = (bf16[256,1536]{1,0:T(8,128)(2,1)}, bf16[256,1152]{1,0:T(8,128)(2,1)}, f32[48,1152]{1,0:T(8,128)}) custom-call(bf16[256,1536]{1,0:T(8,128)(2,1)} %x_ref.1, bf16[48,1152]{1,0:T(8,128)(2,1)} %w_ref.1, bf16[256,1152]{1,0:T(8,128)(2,1)} %t_ref.1, f32[1]{0:T(128)S(6)} %copy.11.lf_ref, f32[1]{0:T(128)S(6)} %copy.12.bias_ref), custom_call_target="tpu_custom_call" | custom-call | tf_op jit(solution)/shard_map/pallas_call | solution.py:398
  84.9 0.0 copy-start
  84.9 2.1 %copy.13 = bf16[256,1536]{1,0:T(8,128)(2,1)} copy(bf16[256,1536]{1,0:T(8,128)(2,1)} %get-tuple-element.6) | data formatting | bytes 1572864
  87.0 0.0 copy-done
  87.0 0.0 copy-start.1
  87.0 0.8 copy.14
  87.8 0.3 copy-done.1
  88.2 0.7 copy.15
Async XLA Ops:
  84.9 2.1 %copy-start = (bf16[256,1152]{1,0:T(8,128)(2,1)S(1)}, bf16[256,1152]{1,0:T(8,128)(2,1)}, u32[]{:S(2)}) copy-start(bf16[256,1152]{1,0:T(8,128)(2,1)} %get-tuple-element.7) | copy-start | bytes 1769476
  87.0 1.1 %copy-start.1 = (f32[48,1152]{1,0:T(8,128)S(1)}, f32[48,1152]{1,0:T(8,128)}, u32[]{:S(2)}) copy-start(f32[48,1152]{1,0:T(8,128)} %get-tuple-element.8) | copy-start | bytes 663556
where the time goes:
time: 89.1 us; the launch traced here: 88.8 us
  Pallas kernels  82.9 us (93%)
  local copies, waits for them, and re-layouts  3.96 us (4%)
  between operations  1.94 us (2%)
    pallas_call x1, Pallas kernels, fused(): pl.pallas_call(functools.partial(kernel, n, axis, keys), out_shape=(jax.S...  82.9 us
    unnamed x7, local copies, waits for them, and re-layouts  3.96 us

commit v1 on v0

v1 whole, which is shorter than its diff:
```python
import functools

import jax
import jax.numpy as jnp
from jax import lax
from jax.experimental import pallas as pl
from jax.experimental.pallas import tpu as pltpu
from jax.sharding import PartitionSpec as P

S = 4
epsilon = 1e-06
MESH = pl.DeviceIdType.MESH
F32 = jnp.float32
BF = jnp.bfloat16


def dot_nt(a, b):
    return lax.dot_general(a, b, (((1,), (1,)), ((), ())), preferred_element_type=F32)


def pair_grad(rows, cols, t, bias, own):
    logits = t * dot_nt(rows, cols) + bias
    if own:
        matched = lax.broadcasted_iota(jnp.int32, logits.shape, 0) == lax.broadcasted_iota(
            jnp.int32, logits.shape, 1
        )
        z = jnp.where(matched, 1.0, -1.0).astype(F32)
        return (-t * z * jax.nn.sigmoid(-z * logits)).astype(BF)
    return (t * jax.nn.sigmoid(logits)).astype(BF)


CHUNKS = 4


def sem_keys():
    keys = ["o1", "o2", "o3", "s2", "s3", "rx", "ry"]
    for p in range(4):
        keys += [("px", p), ("py", p), ("dA", p), ("dB", p), ("zx", p), ("zy", p)]
        keys += [("w", p, i) for i in range(5)]
        keys += [("g0", p), ("gA", p), ("gB", p)]
    keys += ["g1o", "g2o", "g3o", "gs2", "gs3", "gx3", "gy3", "gx0", "gy0"]
    keys += ["g1x", "g1y", "gex", "gey", "g2x", "g2y"]
    for k in ("t", "i"):
        keys += [(k, "own")]
        for kind in ("near", "far", "pass", "first", "second", "relay", "relay2", "onear", "ofar"):
            keys += [(k, kind, c) for c in range(CHUNKS)]
    return {k: i for i, k in enumerate(keys)}


def kernel(
    n, axis, keys,
    x_hbm, w_hbm, t_hbm, lf_hbm, bias_hbm,
    gx_ref, gt_ref, gw_ref,
    x_ref, t_ref, w_all, text_low, text_in, image_low, image_in, xt, gz, from_core, to_core,
    out_s, in_d, in_xy, in_z, in_e,
    factor_ref, bias_ref, load_sem, send_sem, recv_sem,
):
    rows, width = x_ref.shape
    own_rows, cols = w_all.shape[1:]
    ha = (cols // 128 + 1) // 2 * 128
    A, B, FULL = pl.ds(0, ha), pl.ds(ha, cols - ha), pl.ds(0, cols)
    me = lax.axis_index(axis)
    core = lax.rem(me, 2)
    chip = me // 2
    x = lax.rem(chip, 2)
    y = lax.rem(chip // 2, 2)
    z = chip // 4
    side = z // 2
    plane = [z, z + 1 - 2 * lax.rem(z, 2), 2 - side, 3 * (1 - side)]
    inner = lax.rem(z + side, 2) == 1
    outer = jnp.logical_not(inner)
    other = 1 - core

    def dev(z_, y_, x_, c_):
        return ((z_ * 2 + y_) * 2 + x_) * 2 + c_

    xn, yn, partner = dev(z, y, 1 - x, core), dev(z, 1 - y, x, core), dev(z, y, x, other)
    peer = [None] + [dev(plane[p], y, x, core) for p in range(1, 4)]

    def place(r):
        return (y, 1 - y)[r in ("y", "d")], (x, 1 - x)[r in ("x", "d")]

    def shard(p, r, c_=None):
        y_, x_ = place(r)
        return dev(plane[p], y_, x_, core if c_ is None else c_)

    waits = []

    def copy(src, dst, key, target, recv=None):
        i = keys[key]
        return pltpu.make_async_remote_copy(
            src_ref=src, dst_ref=dst, send_sem=send_sem.at[i],
            recv_sem=recv_sem.at[i if recv is None else recv],
            device_id=(target,), device_id_type=MESH,
        )

    def send(src, dst, key, target, recv=None, cond=None):
        c = copy(src, dst, key, target, recv)
        if cond is None:
            c.start()
        else:
            pl.when(cond)(c.start)
        waits.append((cond, c))

    def arrived(dst, key):
        copy(dst, dst, key, partner).wait_recv()

    barrier = pltpu.get_barrier_semaphore()
    peers = [partner, xn, yn] + peer[1:] + [lax.rem(me + n + s, n) for s in (-2, 2, -4, 4)]
    for p in peers:
        pl.semaphore_signal(barrier, inc=1, device_id=(p,), device_id_type=MESH)

    loads = [
        pltpu.make_async_copy(src, dst, load_sem.at[i])
        for i, (src, dst) in enumerate(
            [
                (w_hbm, w_all.at[me]), (t_hbm, t_ref), (lf_hbm, factor_ref), (bias_hbm, bias_ref),
                (x_hbm, x_ref),
            ]
        )
    ]
    for c in loads:
        c.start()
    for c in loads[1:4]:
        c.wait()
    t = jnp.exp(jnp.full((1, 1), factor_ref[0], F32))
    bias = bias_ref[0]
    text = t_ref[...].astype(F32)
    text_length = jnp.sqrt(jnp.sum(text * text, axis=1, keepdims=True) + epsilon)
    text_low[...] = (text / text_length).astype(BF)
    loads[0].wait()

    pl.semaphore_wait(barrier, len(peers))

    def w_at(p, r, cut=FULL):
        return w_all.at[shard(p, r), :, cut]

    def swap(p, r, i, cut=FULL):
        send(w_at(p, r, cut), w_at(p, r, cut), ("w", p, i), partner)

    def onto(p, r, cut, key, target, cond=None, dst_key=None):
        send(w_at(p, r, cut), w_at(p, r, cut), key, target, None if dst_key is None else keys[dst_key], cond)

    far_key = jnp.where(inner, keys["o2"], keys["o3"])
    own = w_all.at[me]
    send(own, own, "s3", peer[3], far_key)
    send(own, own, "s2", peer[2], far_key)
    send(own, own, "o1", peer[1])
    send(own, own, ("px", 0), xn)
    send(own, own, ("py", 0), yn)
    send(own, own, ("w", 0, 0), partner)

    part = rows // CHUNKS

    class Window:
        def __init__(self, key, buf, slots, mirror):
            self.key, self.buf, self.slots = key, buf, slots
            v = n - 1 - me if mirror else me
            self.c = lax.rem(v, 2)
            q = lax.rem(v // 2, 4)
            self.q = q
            step = 2 if mirror else -2
            back = lax.rem(me + n + step, n)
            back2 = lax.rem(me + n + 2 * step, n)
            back4 = lax.rem(me + n + 4 * step, n)
            first_c = self.c == 0
            odd = lax.rem(q, 2) == 1
            even = jnp.logical_not(odd)
            far_first = jnp.logical_and(first_c, even)
            self.first_target = jnp.where(far_first, back2, back)
            self.first_slot = jnp.where(far_first, 3, self.c)
            self.first_kind = jnp.where(far_first, 1, 0)
            self.is_c0 = first_c
            self.is_c1 = jnp.logical_not(first_c)
            self.has_second = jnp.logical_and(first_c, odd)
            passing = q == 1
            self.second_target = jnp.where(passing, back4, back2)
            self.second_slot = jnp.where(passing, 4, 3)
            self.second_kind = jnp.where(passing, 2, 1)
            self.relays = far_first
            self.passes = jnp.logical_and(first_c, passing)

        def rows(self, c):
            return pl.ds(c * part, part)

        def recv(self, kind, c):
            return keys[(self.key, "near", c)] + CHUNKS * kind

        def start(self, c):
            r = self.rows(c)
            send(
                self.buf.at[r], self.slots.at[self.first_slot, r], (self.key, "first", c),
                self.first_target, self.recv(self.first_kind, c),
            )
            send(
                self.buf.at[r], self.slots.at[self.second_slot, r], (self.key, "second", c),
                self.second_target, self.recv(self.second_kind, c), self.has_second,
            )

        def own(self):
            send(self.buf, self.slots.at[2], (self.key, "own"), partner, None, self.is_c1)

        def passed(self, c):
            r = self.rows(c)

            @pl.when(self.passes)
            def _():
                arrived(self.slots.at[4, r], (self.key, "pass", c))

            send(
                self.slots.at[4, r], self.slots.at[3, r], (self.key, "relay2", c), yn,
                self.recv(1, c), self.passes,
            )

        def far(self, c):
            r = self.rows(c)

            @pl.when(self.is_c0)
            def _():
                arrived(self.slots.at[3, r], (self.key, "far", c))

            send(
                self.slots.at[3, r], self.slots.at[0, r], (self.key, "relay", c), xn,
                self.recv(0, c), self.relays,
            )
            send(
                self.slots.at[3, r], self.slots.at[2, r], (self.key, "ofar", c), partner,
                None, self.is_c0,
            )

        def near(self, c):
            r = self.rows(c)
            slot = self.slots.at[self.c, r]
            arrived(slot, (self.key, "near", c))
            send(slot, slot, (self.key, "onear", c), partner)

        def wait_near_partner(self):
            for c in range(CHUNKS):
                arrived(self.slots.at[1 - self.c, self.rows(c)], (self.key, "onear", c))

        def wait_last(self):
            @pl.when(self.is_c0)
            def _():
                arrived(self.slots.at[2], (self.key, "own"))

            @pl.when(self.is_c1)
            def _():
                for c in range(CHUNKS):
                    arrived(self.slots.at[2, self.rows(c)], (self.key, "ofar", c))

    tw = Window("t", text_low, text_in, False)
    iw = Window("i", image_low, image_in, True)

    def got_plane(p):
        arrived(w_at(p, "d", A), ("dA", p))
        swap(p, "d", 3, A)
        arrived(w_at(p, "d", B), ("dB", p))
        swap(p, "d", 4, B)

    def side_x(p, key):
        arrived(w_at(p, "x"), key)
        onto(p, "x", A, ("dA", p), yn)

    def side_y(p, key):
        arrived(w_at(p, "y"), key)
        onto(p, "y", B, ("dB", p), xn)

    tw.own()
    tw.start(0)
    side_x(0, ("px", 0))
    onto(0, "x", FULL, ("zx", 1), peer[1])
    onto(0, "x", FULL, ("zx", 2), peer[2], inner)
    swap(0, "x", 1)
    side_y(0, ("py", 0))
    onto(0, "y", FULL, ("zy", 1), peer[1])
    onto(0, "y", FULL, ("zy", 2), peer[2], inner)
    swap(0, "y", 2)
    tw.start(1)
    arrived(w_at(3, "o"), "o3")
    onto(3, "o", FULL, ("px", 3), xn)
    onto(3, "o", FULL, ("py", 3), yn)
    tw.start(2)
    swap(3, "o", 0)
    arrived(w_at(1, "o"), "o1")
    swap(1, "o", 0)
    arrived(w_at(2, "o"), "o2")
    swap(2, "o", 0)
    got_plane(0)
    tw.passed(0)
    tw.far(0)
    tw.start(3)
    side_x(1, ("zx", 1))
    swap(1, "x", 1)
    side_y(1, ("zy", 1))
    swap(1, "y", 2)
    tw.passed(1)
    tw.far(1)
    side_x(3, ("px", 3))
    swap(3, "x", 1)
    side_y(3, ("py", 3))
    swap(3, "y", 2)
    tw.passed(2)
    tw.far(2)
    side_x(2, ("zx", 2))
    onto(2, "x", FULL, "rx", peer[1], inner, ("zx", 2))
    swap(2, "x", 1)
    side_y(2, ("zy", 2))
    onto(2, "y", FULL, "ry", peer[1], inner, ("zy", 2))
    swap(2, "y", 2)
    got_plane(1)
    got_plane(3)
    tw.passed(3)
    tw.far(3)
    got_plane(2)
    loads[4].wait()
    xt[...] = x_ref[...].T

    for p in range(4):
        for i, (r, cut) in enumerate([("o", FULL), ("x", FULL), ("y", FULL), ("d", A), ("d", B)]):
            arrived(w_all.at[shard(p, r, other), :, cut], ("w", p, i))

    weight = w_all[...].reshape(n * own_rows, cols)
    embedded = jnp.dot(x_ref[...], weight, preferred_element_type=F32)
    image_length = jnp.sqrt(jnp.sum(embedded * embedded, axis=1, keepdims=True) + epsilon)
    image_unit = embedded / image_length
    image_low[...] = image_unit.astype(BF)
    iw.own()
    for c in range(CHUNKS):
        iw.start(c)
    mine = image_low[...]
    own_text = text_low[...]
    grad = pair_grad(mine, own_text, t, bias, True)
    image_grad = jnp.dot(grad, own_text, preferred_element_type=F32)

    for c in range(CHUNKS):
        tw.near(c)

    def window(low, win, grads):
        for q in (2, 0, 1):
            if q == 2:
                win.wait_last()
            if q == 0:
                win.wait_near_partner()
            block = win.slots[q]
            grads += jnp.dot(
                pair_grad(low, block, t, bias, False), block, preferred_element_type=F32
            )
        return grads

    image_grad = window(mine, tw, image_grad)
    iw.passed(0)
    iw.far(0)
    along = jnp.sum(image_unit * image_grad, axis=1, keepdims=True)
    embed_grad = ((image_grad - image_unit * along) / image_length).astype(BF)

    def spot(p, r):
        y_, x_ = place(r)
        return y_ * 2 + x_

    group = 8 * own_rows
    for p in (3, 2, 1, 0):
        lhs = xt[pl.ds(pl.multiple_of(plane[p] * group, group), group), :]
        product = jnp.dot(lhs, embed_grad, preferred_element_type=F32)
        gz[p] = product.reshape(4, 2, own_rows, cols)
        for c in range(4):
            to_core[p, c] = gz[p, c, other].astype(BF)
        send(to_core.at[p], from_core.at[p], ("g0", p), partner)

    S_O, S_X, S_Y, S_D = range(4)

    def base(p, r, cut):
        c = spot(p, r)
        return gz[p, c, core, :, cut] + from_core[p, c, :, cut].astype(F32)

    def put(p, r, cut, value):
        out_s[p, r, :, cut] = value.astype(BF)

    def open_plane(p):
        arrived(from_core.at[p], ("g0", p))
        put(p, S_D, FULL, base(p, "d", FULL))
        send(out_s.at[p, S_D, :, A], in_d.at[p, :, A], ("gA", p), yn)
        send(out_s.at[p, S_D, :, B], in_d.at[p, :, B], ("gB", p), xn)

    gs_key = jnp.where(inner, keys["g2o"], keys["g3o"])
    gs_slot = jnp.where(inner, 1, 2)

    def sides(p):
        arrived(in_d.at[p, :, A], ("gA", p))
        arrived(in_d.at[p, :, B], ("gB", p))

    def x_sum(p, cut):
        v = base(p, "x", cut)
        return v + in_d[p, :, cut].astype(F32) if cut is A else v

    def y_sum(p, cut):
        v = base(p, "y", cut)
        return v + in_d[p, :, cut].astype(F32) if cut is B else v

    open_plane(3)
    open_plane(2)
    iw.passed(1)
    iw.far(1)
    put(2, S_O, FULL, base(2, "o", FULL))
    send(out_s.at[2, S_O], in_z.at[gs_slot, 0], "gs2", peer[2], gs_key)
    open_plane(1)
    iw.passed(2)
    iw.far(2)
    put(1, S_O, FULL, base(1, "o", FULL))
    send(out_s.at[1, S_O], in_z.at[0, 0], "g1o", peer[1])
    sides(3)
    for cut in (A, B):
        put(3, S_X, cut, x_sum(3, cut))
        put(3, S_Y, cut, y_sum(3, cut))
    send(out_s.at[3, S_X], in_xy.at[1, 0], "gx3", xn)
    send(out_s.at[3, S_Y], in_xy.at[1, 1], "gy3", yn)
    iw.passed(3)
    iw.far(3)
    open_plane(0)
    sides(2)
    for cut in (A, B):
        put(2, S_X, cut, x_sum(2, cut))
        put(2, S_Y, cut, y_sum(2, cut))

    @pl.when(outer)
    def _():
        copy(out_s.at[2, S_X], in_e.at[0], "gex", peer[1]).start()
        copy(out_s.at[2, S_Y], in_e.at[1], "gey", peer[1]).start()

    sides(1)
    for cut in (A, B):
        put(1, S_X, cut, x_sum(1, cut))
        put(1, S_Y, cut, y_sum(1, cut))
    send(out_s.at[1, S_X], in_z.at[0, 1], "g1x", peer[1])
    send(out_s.at[1, S_Y], in_z.at[0, 2], "g1y", peer[1])

    gx_ref[...] = dot_nt(embed_grad, weight).astype(BF)

    @pl.when(inner)
    def _():
        for r, key, fill in ((S_X, "gex", x_sum), (S_Y, "gey", y_sum)):
            arrived(in_e.at[r - 1], key)
            for cut in (A, B):
                put(2, r, cut, fill(2, cut) + in_e[r - 1, :, cut].astype(F32))
            copy(out_s.at[2, r], in_z.at[1, r], ("g2x", "g2y")[r - 1], peer[2]).start()

    arrived(in_xy.at[1, 0], "gx3")
    arrived(in_xy.at[1, 1], "gy3")
    put(
        3, S_O, FULL,
        base(3, "o", FULL) + in_xy[1, 0].astype(F32) + in_xy[1, 1].astype(F32),
    )
    send(out_s.at[3, S_O], in_z.at[gs_slot, 0], "gs3", peer[3], gs_key)

    text_grad = jnp.dot(
        pair_grad(own_text, mine, t, bias, True), mine, preferred_element_type=F32
    )
    for c in range(CHUNKS):
        iw.near(c)

    sides(0)
    arrived(in_z.at[0, 1], "g1x")
    arrived(in_z.at[0, 2], "g1y")

    @pl.when(outer)
    def _():
        for cut in (A, B):
            put(0, S_X, cut, x_sum(0, cut) + in_z[0, 1, :, cut].astype(F32))
            put(0, S_Y, cut, y_sum(0, cut) + in_z[0, 2, :, cut].astype(F32))

    @pl.when(inner)
    def _():
        arrived(in_z.at[1, 1], "g2x")
        arrived(in_z.at[1, 2], "g2y")
        for cut in (A, B):
            for r, fill in ((1, x_sum), (2, y_sum)):
                put(
                    0, r, cut,
                    fill(0, cut) + in_z[0, r, :, cut].astype(F32) + in_z[1, r, :, cut].astype(F32),
                )

    send(out_s.at[0, S_X], in_xy.at[0, 0], "gx0", xn)
    send(out_s.at[0, S_Y], in_xy.at[0, 1], "gy0", yn)

    text_grad = window(own_text, iw, text_grad)
    text_unit = t_ref[...].astype(F32) / text_length
    along = jnp.sum(text_unit * text_grad, axis=1, keepdims=True)
    gt_ref[...] = ((text_grad - text_unit * along) / text_length).astype(BF)

    total = base(0, "o", FULL)
    for i, key in enumerate(("g1o", "g2o", "g3o")):
        arrived(in_z.at[i, 0], key)
        total += in_z[i, 0].astype(F32)
    gw_ref[...] = total
    arrived(in_xy.at[0, 0], "gx0")
    arrived(in_xy.at[0, 1], "gy0")
    gw_ref[...] += in_xy[0, 0].astype(F32) + in_xy[0, 1].astype(F32)

    for cond, c in waits:
        if cond is None:
            c.wait_send()
        else:
            pl.when(cond)(c.wait_send)

    @pl.when(outer)
    def _():
        copy(out_s.at[2, S_X], in_e.at[0], "gex", peer[1]).wait_send()
        copy(out_s.at[2, S_Y], in_e.at[1], "gey", peer[1]).wait_send()

    @pl.when(inner)
    def _():
        copy(out_s.at[2, S_X], in_z.at[1, 1], "g2x", peer[2]).wait_send()
        copy(out_s.at[2, S_Y], in_z.at[1, 2], "g2y", peer[2]).wait_send()


def fused(n, axis, image_features, head_weight, text_embeds, factor, bias):
    rows, width = image_features.shape
    own_rows, cols = head_weight.shape
    keys = sem_keys()
    hbm = pl.BlockSpec(memory_space=pltpu.HBM)
    vmem = pl.BlockSpec(memory_space=pltpu.VMEM)
    scratch = [
        ((rows, width), BF),
        ((rows, cols), BF),
        ((n, own_rows, cols), BF),
        ((rows, cols), BF),
        ((5, rows, cols), BF),
        ((rows, cols), BF),
        ((5, rows, cols), BF),
        ((width, rows), BF),
        ((4, 4, 2, own_rows, cols), F32),
        ((4, 4, own_rows, cols), BF),
        ((4, 4, own_rows, cols), BF),
        ((4, 4, own_rows, cols), BF),
        ((4, own_rows, cols), BF),
        ((2, 2, own_rows, cols), BF),
        ((3, 3, own_rows, cols), BF),
        ((2, own_rows, cols), BF),
    ]
    results = pl.pallas_call(
        functools.partial(kernel, n, axis, keys),
        out_shape=(
            pltpu.VMEM((rows, width), BF),
            pltpu.VMEM((rows, cols), BF),
            pltpu.VMEM((own_rows, cols), F32),
        ),
        in_specs=[hbm] * 5,
        out_specs=(vmem, vmem, vmem),
        scratch_shapes=[pltpu.VMEM(s, d) for s, d in scratch]
        + [pltpu.SMEM((1,), F32)] * 2
        + [pltpu.SemaphoreType.DMA((5,))]
        + [pltpu.SemaphoreType.DMA((len(keys),))] * 2,
        compiler_params=pltpu.CompilerParams(
            collective_id=0, has_side_effects=True, vmem_limit_bytes=65413120
        ),
    )(image_features, head_weight, text_embeds, factor, bias)
    return pl.pallas_call(
        write_out,
        out_shape=(
            jax.ShapeDtypeStruct((rows, width), BF),
            jax.ShapeDtypeStruct((rows, cols), BF),
            jax.ShapeDtypeStruct((own_rows, cols), F32),
        ),
        in_specs=[vmem] * 3,
        out_specs=(hbm,) * 3,
        scratch_shapes=[pltpu.SemaphoreType.DMA((3,))],
        compiler_params=pltpu.CompilerParams(vmem_limit_bytes=2**20),
    )(*results)


def write_out(gx, gt, gw, gx_out, gt_out, gw_out, sems):
    pairs = ((gx, gx_out), (gt, gt_out), (gw, gw_out))
    copies = [pltpu.make_async_copy(a, b, sems.at[i]) for i, (a, b) in enumerate(pairs)]
    for c in copies:
        c.start()
    for c in copies:
        c.wait()


def passed_along(block, axis, distance):
    devices = range(lax.axis_size(axis))
    route = [((i - distance) % len(devices), i) for i in devices]
    return lax.ppermute(block, axis, route)


def normalize(rows):
    squares = jnp.sum(rows * rows, axis=1, keepdims=True)
    length = jnp.sqrt(squares + epsilon)
    return (rows / length, length)


def similarity_derivative(
    picture_sample_group,
    caption_sample_group,
    similarity_multiplier,
    neighbour_distance,
    outer_dimension_size,
):
    similarity_matrix = (
        similarity_multiplier
        * lax.dot_general(
            picture_sample_group,
            caption_sample_group,
            (((1,), (1,)), ((), ())),
            preferred_element_type=jnp.float32,
        )
        + neighbour_distance
    )
    if outer_dimension_size:
        matched = lax.broadcasted_iota(
            jnp.int32, similarity_matrix.shape, 0
        ) == lax.broadcasted_iota(jnp.int32, similarity_matrix.shape, 1)
        match_polarity = jnp.where(matched, 1.0, -1.0).astype(jnp.float32)
    else:
        match_polarity = -jnp.ones(similarity_matrix.shape, jnp.float32)
    return (
        -similarity_multiplier
        * match_polarity
        * jax.nn.sigmoid(-match_polarity * similarity_matrix)
    ).astype(jnp.bfloat16)


def project_back(grad, unit_rows, length):
    return (grad - unit_rows * jnp.sum(unit_rows * grad, axis=1, keepdims=True)) / length


def by_collectives(image_features, head_weight, text_embeds, natural_exponent_factor, logit_bias):
    full_weight = lax.all_gather(head_weight, "blk", axis=0, tiled=True)
    embedded = jnp.dot(image_features, full_weight, preferred_element_type=jnp.float32)
    image_unit, image_length = normalize(embedded)
    picture_embedding_mapped = image_unit.astype(jnp.bfloat16)
    text_unit, text_length = normalize(text_embeds.astype(jnp.float32))
    text_low = text_unit.astype(jnp.bfloat16)
    similarity_multiplier = jnp.exp(natural_exponent_factor[0])
    neighbour_distance = logit_bias[0]
    image_grad = jnp.zeros(image_unit.shape, jnp.float32)
    current_neighbour_tile = text_low
    for partition_portion in range(S):
        mapping_matrix = similarity_derivative(
            picture_embedding_mapped,
            current_neighbour_tile,
            similarity_multiplier,
            neighbour_distance,
            partition_portion == 0,
        )
        image_grad = image_grad + jnp.dot(
            mapping_matrix, current_neighbour_tile, preferred_element_type=jnp.float32
        )
        if partition_portion + 1 < S:
            current_neighbour_tile = passed_along(current_neighbour_tile, "blk", -1)
    text_grad = jnp.zeros(text_unit.shape, jnp.float32)
    passing = picture_embedding_mapped
    for partition_portion in range(S):
        mapping_matrix = similarity_derivative(
            passing, text_low, similarity_multiplier, neighbour_distance, partition_portion == 0
        )
        text_grad = text_grad + lax.dot_general(
            mapping_matrix, passing, (((0,), (0,)), ((), ())), preferred_element_type=jnp.float32
        )
        if partition_portion + 1 < S:
            passing = passed_along(passing, "blk", 1)
    embed_grad = project_back(image_grad, image_unit, image_length).astype(jnp.bfloat16)
    grad_text = project_back(text_grad, text_unit, text_length).astype(jnp.bfloat16)
    grad_features = lax.dot_general(
        embed_grad, full_weight, (((1,), (1,)), ((), ())), preferred_element_type=jnp.float32
    ).astype(jnp.bfloat16)
    grad_weight = lax.psum_scatter(
        lax.dot_general(
            image_features, embed_grad, (((0,), (0,)), ((), ())), preferred_element_type=jnp.float32
        ),
        "blk",
        scatter_dimension=0,
        tiled=True,
    )
    return (grad_features, grad_text, grad_weight)


def on_device(image_features, head_weight, text_embeds, natural_exponent_factor, logit_bias):
    n = lax.axis_size("blk")
    whole_tiles = head_weight.shape[0] % 16 == 0 and n % 8 == 0 and n // 8 == 4
    run = functools.partial(fused, n, "blk") if whole_tiles else by_collectives
    return run(image_features, head_weight, text_embeds, natural_exponent_factor, logit_bias)


def solution(mesh):
    return jax.shard_map(
        on_device,
        mesh=mesh,
        in_specs=(P("blk", None), P("blk", None), P("blk", None), P(), P()),
        out_specs=(P("blk", None), P("blk", None), P("blk", None)),
        check_vma=False,
    )
```

time: 89.1 us -> 81.7 us (0.917)
  the two profiles are of different devices: /device:TPU:0 before, /device:TPU:16 now
where the time goes in v1:
time: 81.7 us; the launch traced here: 81.6 us
  Pallas kernels  79.6 us (97%)
  between operations  1.93 us (2%)
    pallas_call x1, Pallas kernels, fused(): pl.pallas_call(functools.partial(kernel, n, axis, keys), out_shape=(pltpu...  78.5 us

profile of v1, /device:TPU:16, one launch (start us, length us, event | category | flops | bytes accessed | tf_op | source)
XLA Modules:
  0.0 81.6 jit_solution(7802324316608605952)
XLA Ops:
  1.9 78.5 %shard_map.76 = (bf16[256,1536]{1,0:T(8,128)(2,1)S(1)}, bf16[256,1152]{1,0:T(8,128)(2,1)S(1)}, f32[48,1152]{1,0:T(8,128)S(1)}) custom-call(bf16[256,1536]{1,0:T(8,128)(2,1)} %x_hbm.1, bf16[48,1152]{1,0:T(8,128)(2,1)} %w_hbm.1, bf16[256,1152]{1,0:T(8,128)(2,1)} %t_hbm.1, f32[1]{0:T(128)S(6)} %copy.8.lf_hbm, f32[1]{0:T(128)S(6)} %copy.9.bias_hbm), custom_call_target="tpu_custom_call" | custom-call | tf_op jit(solution)/shard_map/pallas_call | solution.py:539
  80.4 1.2 %shard_map.77 = (bf16[256,1536]{1,0:T(8,128)(2,1)}, bf16[256,1152]{1,0:T(8,128)(2,1)}, f32[48,1152]{1,0:T(8,128)}) custom-call(bf16[256,1536]{1,0:T(8,128)(2,1)S(1)} %get-tuple-element.6.gx, bf16[256,1152]{1,0:T(8,128)(2,1)S(1)} %get-tuple-element.7.gt, f32[48,1152]{1,0:T(8,128)S(1)} %get-tuple-element.8.gw), custom_call_target="tpu_custom_call" | custom-call | tf_op jit(solution)/shard_map/pallas_call | solution.py:556

commit v2 on v1

v2 whole, which is shorter than its diff:
```python
import functools

import jax
import jax.numpy as jnp
from jax import lax
from jax.experimental import pallas as pl
from jax.experimental.pallas import tpu as pltpu
from jax.sharding import PartitionSpec as P

S = 4
epsilon = 1e-06
MESH = pl.DeviceIdType.MESH
F32 = jnp.float32
BF = jnp.bfloat16


def dot_nt(a, b):
    return lax.dot_general(a, b, (((1,), (1,)), ((), ())), preferred_element_type=F32)


def pair_grad(rows, cols, t, bias, own):
    logits = t * dot_nt(rows, cols) + bias
    if own:
        matched = lax.broadcasted_iota(jnp.int32, logits.shape, 0) == lax.broadcasted_iota(
            jnp.int32, logits.shape, 1
        )
        z = jnp.where(matched, 1.0, -1.0).astype(F32)
        return (-t * z * jax.nn.sigmoid(-z * logits)).astype(BF)
    return (t * jax.nn.sigmoid(logits)).astype(BF)


CHUNKS = 4
SENDS = 16
RECVS = 48


class Keys(dict):
    def __missing__(self, key):
        self[key] = len(self)
        return self[key]


def kernel(
    n, axis,
    x_hbm, w_hbm, t_hbm, scalars,
    gx_ref, gt_ref, gw_ref,
    x_ref, t_ref, w_all, text_low, text_in, image_low, image_in, xt, gz, from_core, to_core,
    out_s, in_d, in_xy, in_z, in_e, in_fin, pre_out, pre_in, embedded_ref,
    load_sem, send_sem, recv_sem, credit,
):
    rows, width = x_ref.shape
    own_rows, cols = w_all.shape[1:]
    ha = (cols // 128 + 1) // 2 * 128
    A, B, FULL = pl.ds(0, ha), pl.ds(ha, cols - ha), pl.ds(0, cols)
    me = lax.axis_index(axis)
    core = lax.rem(me, 2)
    chip = me // 2
    x = lax.rem(chip, 2)
    y = lax.rem(chip // 2, 2)
    z = chip // 4
    side = z // 2
    plane = [z, z + 1 - 2 * lax.rem(z, 2), 2 - side, 3 * (1 - side)]
    inner = lax.rem(z + side, 2) == 1
    outer = jnp.logical_not(inner)
    hub = core == 0
    lead = core == 1
    sends = (Keys(), Keys())
    recvs = (Keys(), Keys())

    def dev(z_, y_, x_, c_):
        return ((z_ * 2 + y_) * 2 + x_) * 2 + c_

    def xn(c_):
        return dev(z, y, 1 - x, c_)

    def yn(c_):
        return dev(z, 1 - y, x, c_)

    def peer(p, c_):
        return dev(plane[p], y, x, c_)

    partner = dev(z, y, x, 1 - core)

    def send(src, dst, role, key, to_role, recv, target, cond=None):
        c = pltpu.make_async_remote_copy(
            src_ref=src, dst_ref=dst, send_sem=send_sem.at[sends[role][key]],
            recv_sem=recv_sem.at[recv if not isinstance(recv, (str, tuple)) else recvs[to_role][recv]],
            device_id=(target,), device_id_type=MESH,
        )
        if cond is None:
            c.start()
        else:
            pl.when(cond)(c.start)

    def arrived(ref, role, key):
        pltpu.make_async_remote_copy(
            src_ref=ref, dst_ref=ref, send_sem=send_sem.at[0],
            recv_sem=recv_sem.at[recvs[role][key]],
            device_id=(partner,), device_id_type=MESH,
        ).wait_recv()

    def drained(ref, role, key):
        pltpu.make_async_remote_copy(
            src_ref=ref, dst_ref=ref, send_sem=send_sem.at[sends[role][key]],
            recv_sem=recv_sem.at[0], device_id=(partner,), device_id_type=MESH,
        ).wait_send()

    def shards(count):
        return w_all.at[pl.ds(0, count)]

    barrier = pltpu.get_barrier_semaphore()
    peers = [partner]
    for c in range(2):
        peers += [xn(c), yn(c)] + [peer(p, c) for p in range(1, 4)]
    peers += [lax.rem(me + n + s, n) for s in (-2, 2, -4, 4)]
    for p in peers:
        pl.semaphore_signal(barrier, inc=1, device_id=(p,), device_id_type=MESH)

    pairs = [
        (w_hbm, w_all.at[me]), (t_hbm, t_ref),
        (x_hbm, x_ref),
    ]
    loads = [pltpu.make_async_copy(a, b, load_sem.at[i]) for i, (a, b) in enumerate(pairs)]
    for c in loads:
        c.start()
    for c in loads[1:2]:
        c.wait()
    t = jnp.exp(jnp.full((1, 1), scalars[0], F32))
    bias = scalars[1]
    text = t_ref[...].astype(F32)
    text_length = jnp.sqrt(jnp.sum(text * text, axis=1, keepdims=True) + epsilon)
    text_low[...] = (text / text_length).astype(BF)
    loads[0].wait()

    pl.semaphore_wait(barrier, len(peers))

    part = rows // CHUNKS

    def cut_rows(c):
        return pl.ds(c * part, part)

    class Window:
        def __init__(self, key, buf, slots, mirror):
            self.key, self.buf, self.slots, self.mirror = key, buf, slots, mirror
            v = n - 1 - me if mirror else me
            q = lax.rem(v // 2, 4)
            step = 2 if mirror else -2
            back = lax.rem(me + n + step, n)
            back2 = lax.rem(me + n + 2 * step, n)
            self.back = back
            odd = lax.rem(q, 2) == 1
            even = jnp.logical_not(odd)
            self.odd, self.even, self.back2 = odd, even, back2
            self.leaf_third = 2 if mirror else 3
            self.low, self.high = slots.at[2], buf
            if not mirror:
                self.low, self.high = buf, slots.at[2]

        def at(self, slot, c):
            return self.slots.at[slot, cut_rows(c)]

        def leaf_sends(self):
            send(self.buf, self.slots.at[2], 1, (self.key, "own"), 0, (self.key, "own"), partner)

        def hub_own(self):
            send(self.buf, self.slots.at[2], 0, (self.key, "all"), 1, (self.key, "third"), partner)

        def wait_own(self):
            arrived(self.slots.at[2], 0, (self.key, "own"))

        def start_low(self, c):
            r = cut_rows(c)
            send(
                self.low.at[r], self.at(3, c), 0, (self.key, "all"), 0,
                (self.key, 3, c), self.back2,
            )
            send(
                self.low.at[r], self.at(0, c), 0, (self.key, "mixed"), 0,
                (self.key, 0, c), self.back, self.odd,
            )

        def start_high(self, c):
            r = cut_rows(c)
            send(
                self.high.at[r], self.at(1, c), 0, (self.key, "all"), 0,
                (self.key, 1, c), self.back,
            )

        def far(self, c):
            arrived(self.at(3, c), 0, (self.key, 3, c))
            send(
                self.at(3, c), self.at(0, c), 0, (self.key, "mixed"), 0,
                (self.key, 0, c), xn(0), self.even,
            )
            if not self.mirror:
                send(
                    self.at(3, c), self.at(3, c), 0, (self.key, "all"), 1,
                    (self.key, "third"), partner,
                )

        def near(self, slot, c):
            arrived(self.at(slot, c), 0, (self.key, slot, c))
            send(
                self.at(slot, c), self.at(slot, c), 0, (self.key, "all"), 1,
                (self.key, slot), partner,
            )

        def third(self):
            return 3 - core if self.mirror else 2 + core

        def leaf_wait(self, slot):
            arrived(self.slots.at[slot], 1, (self.key, slot if slot < 2 else "third"))

        def drain(self):
            @pl.when(hub)
            def _():
                drained(self.slots, 0, (self.key, "all"))
                drained(self.slots.at[0], 0, (self.key, "mixed"))

            @pl.when(lead)
            def _():
                drained(self.slots.at[0], 1, (self.key, "own"))

    def release():
        pl.semaphore_signal(credit, inc=1, device_id=(partner,), device_id_type=MESH)

    tw = Window("t", text_low, text_in, False)
    iw = Window("i", image_low, image_in, True)

    def place(r):
        return (y, 1 - y)[r in ("y", "d")], (x, 1 - x)[r in ("x", "d")]

    def pair(p, r, cut=FULL):
        y_, x_ = place(r)
        return w_all.at[pl.ds(pl.multiple_of(dev(plane[p], y_, x_, 0), 2), 2), :, cut]

    for key in ("o1", "o2", "o3", "px0", "py0"):
        recvs[1][key]
    far_key = jnp.where(inner, recvs[1]["o2"], recvs[1]["o3"])
    own = w_all.at[me]

    def wait_pair(p, r, key):
        arrived(pair(p, r), 1, key)
        send(pair(p, r), pair(p, r), 1, "w", 0, ("w", p), partner)

    def onto(p, r, cut, recv, target, key="ag", cond=None):
        send(pair(p, r, cut), pair(p, r, cut), 1, key, 1, recv, target, cond)

    def diagonal(p):
        wait_pair(p, "d", ("d", p))

    def side_x(p, key):
        arrived(pair(p, "x"), 1, key)
        onto(p, "x", A, ("d", p), yn(1))

    def side_y(p, key):
        arrived(pair(p, "y"), 1, key)
        onto(p, "y", B, ("d", p), xn(1))

    def swap(p, r):
        send(pair(p, r), pair(p, r), 1, "w", 0, ("w", p), partner)

    def first_sends(role):
        for target, recv in (
            (peer(3, 1), far_key), (peer(2, 1), far_key), (peer(1, 1), "o1"),
            (xn(1), "px0"), (yn(1), "py0"),
        ):
            send(own, own, role, "ag", 1, recv, target)

    @pl.when(hub)
    def _():
        first_sends(0)
        send(own, own, 0, "ag", 1, "w0", partner)
        tw.start_low(0)
        tw.wait_own()
        tw.start_high(0)
        for c in range(1, CHUNKS):
            pl.semaphore_wait(credit, 1)
            tw.start_low(c)
            tw.start_high(c)
        for c in range(CHUNKS):
            tw.far(c)

    @pl.when(lead)
    def _():
        first_sends(1)
        send(own, own, 1, "w", 0, ("w", 0), partner)
        tw.leaf_sends()

        side_x(0, "px0")
        onto(0, "x", FULL, ("zx", 1), peer(1, 1))
        onto(0, "x", FULL, ("zx", 2), peer(2, 1), "ag", inner)
        swap(0, "x")
        side_y(0, "py0")
        onto(0, "y", FULL, ("zy", 1), peer(1, 1))
        onto(0, "y", FULL, ("zy", 2), peer(2, 1), "ag", inner)
        swap(0, "y")
        arrived(pair(3, "o"), 1, "o3")
        onto(3, "o", FULL, "px3", xn(1))
        onto(3, "o", FULL, "py3", yn(1))
        swap(3, "o")
        arrived(pair(2, "o"), 1, "o2")
        onto(2, "o", FULL, ("zx", 2), xn(1), "ag", outer)
        onto(2, "o", FULL, ("zy", 2), yn(1), "ag", outer)
        swap(2, "o")
        wait_pair(1, "o", "o1")
        release()
        diagonal(0)
        side_x(1, ("zx", 1))
        swap(1, "x")
        side_y(1, ("zy", 1))
        swap(1, "y")
        release()
        side_x(3, "px3")
        swap(3, "x")
        side_y(3, "py3")
        swap(3, "y")
        release()
        side_x(2, ("zx", 2))
        swap(2, "x")
        side_y(2, ("zy", 2))
        swap(2, "y")
        diagonal(1)

    loads[2].wait()
    xt[...] = x_ref[...].T

    @pl.when(hub)
    def _():
        arrived(shards(7), 0, ("w", 0))
        arrived(shards(8), 0, ("w", 1))

    def project(p):
        at = pl.ds(pl.multiple_of(plane[p] * 8 * own_rows, 8 * own_rows), 8 * own_rows)
        rows_of = w_all[pl.ds(pl.multiple_of(plane[p] * 8, 8), 8)].reshape(8 * own_rows, cols)
        return jnp.dot(x_ref[:, at], rows_of, preferred_element_type=F32)

    @pl.when(lead)
    def _():
        arrived(w_all.at[partner], 1, "w0")

    embedded_ref[...] = project(0)
    embedded_ref[...] += project(1)

    @pl.when(hub)
    def _():
        for c in range(CHUNKS):
            tw.near(1, c)
        arrived(shards(8), 0, ("w", 3))

    @pl.when(lead)
    def _():
        diagonal(3)

    embedded_ref[...] += project(3)

    @pl.when(hub)
    def _():
        for c in range(CHUNKS):
            tw.near(0, c)
        arrived(shards(8), 0, ("w", 2))

    @pl.when(lead)
    def _():
        diagonal(2)

    weight = w_all[...].reshape(n * own_rows, cols)
    embedded = embedded_ref[...] + project(2)
    image_length = jnp.sqrt(jnp.sum(embedded * embedded, axis=1, keepdims=True) + epsilon)
    image_unit = embedded / image_length
    image_low[...] = image_unit.astype(BF)

    @pl.when(hub)
    def _():
        iw.hub_own()
        for c in range(3):
            iw.start_high(c)

    @pl.when(lead)
    def _():
        iw.leaf_sends()

    mine = image_low[...]
    own_text = text_low[...]
    grad = pair_grad(mine, own_text, t, bias, True)
    image_grad = jnp.dot(grad, own_text, preferred_element_type=F32)

    @pl.when(hub)
    def _():
        iw.wait_own()
        for c in range(3):
            iw.start_low(c)

    def window(low, win, grads):
        for i, q in enumerate((win.third(), 1, 0)):
            @pl.when(lead)
            def _():
                win.leaf_wait((win.leaf_third, 1, 0)[i])

            block = win.slots[q]
            grads += jnp.dot(
                pair_grad(low, block, t, bias, False), block, preferred_element_type=F32
            )
        return grads

    image_grad = window(mine, tw, image_grad)
    along = jnp.sum(image_unit * image_grad, axis=1, keepdims=True)
    embed_grad = ((image_grad - image_unit * along) / image_length).astype(BF)

    def hand_over(p, r):
        y_, x_ = place(r)
        c = y_ * 2 + x_
        key = ("g0", p, "d" if r == "d" else "rest")
        send(to_core.at[p, c], from_core.at[p, c], 0, "g0", 1, key, partner)

    group = 8 * own_rows
    for p in (3, 2, 1, 0):
        lhs = xt[pl.ds(pl.multiple_of(plane[p] * group, group), group), :]
        product = jnp.dot(lhs, embed_grad, preferred_element_type=F32)
        gz[p] = product.reshape(4, 2, own_rows, cols)

        @pl.when(hub)
        def _():
            to_core[p] = gz[p].astype(BF)
            hand_over(p, "d")

    @pl.when(hub)
    def _():
        for p in (3, 2, 1, 0):
            for r in ("x", "y", "o"):
                hand_over(p, r)

    S_O, S_X, S_Y, S_D = range(4)

    def base(p, r, cut):
        y_, x_ = place(r)
        c = y_ * 2 + x_
        return gz[p, c, :, :, cut] + from_core[p, c, :, :, cut].astype(F32)

    def put(p, r, cut, value):
        out_s[p, r, :, :, cut] = value.astype(BF)

    def open_plane(p):
        arrived(from_core.at[p, 0], 1, ("g0", p, "d"))
        put(p, S_D, FULL, base(p, "d", FULL))
        send(out_s.at[p, S_D, :, :, A], in_d.at[p, :, :, A], 1, "rs", 1, ("gd", p), yn(1))
        send(out_s.at[p, S_D, :, :, B], in_d.at[p, :, :, B], 1, "rs", 1, ("gd", p), xn(1))

    for key in ("g1o", "g2o", "g3o"):
        recvs[1][key]
    gs_key = jnp.where(inner, recvs[1]["g2o"], recvs[1]["g3o"])
    gs_slot = jnp.where(inner, 1, 2)

    def rest(p):
        arrived(from_core.at[p, pl.ds(0, 3)], 1, ("g0", p, "rest"))

    def sides(p):
        arrived(in_d.at[p], 1, ("gd", p))

    def x_sum(p, cut):
        v = base(p, "x", cut)
        return v + in_d[p, :, :, cut].astype(F32) if cut is A else v

    def y_sum(p, cut):
        v = base(p, "y", cut)
        return v + in_d[p, :, :, cut].astype(F32) if cut is B else v

    def fill_sides(p):
        sides(p)
        for cut in (A, B):
            put(p, S_X, cut, x_sum(p, cut))
            put(p, S_Y, cut, y_sum(p, cut))

    @pl.when(lead)
    def _():
        open_plane(3)
        open_plane(2)
        open_plane(1)
        rest(3)
        rest(2)

        @pl.when(inner)
        def _():
            put(2, S_O, FULL, base(2, "o", FULL))
            send(out_s.at[2, S_O], in_z.at[gs_slot, 0], 1, "rs", 1, gs_key, peer(2, 1))

        rest(1)
        put(1, S_O, FULL, base(1, "o", FULL))
        send(out_s.at[1, S_O], in_z.at[0, 0], 1, "rs", 1, "g1o", peer(1, 1))
        fill_sides(3)
        send(out_s.at[3, S_X], in_xy.at[0], 1, "rs", 1, "gxy3", xn(1))
        send(out_s.at[3, S_Y], in_xy.at[1], 1, "rs", 1, "gxy3", yn(1))
        release()
        open_plane(0)
        rest(0)

    @pl.when(hub)
    def _():
        for c in range(3):
            iw.far(c)
        for c in range(3, CHUNKS):
            pl.semaphore_wait(credit, 1)
            iw.start_low(c)
            iw.start_high(c)
        for c in range(3, CHUNKS):
            iw.far(c)
        for c in range(CHUNKS):
            iw.near(1, c)
        for c in range(CHUNKS):
            iw.near(0, c)

    @pl.when(lead)
    def _():
        fill_sides(2)

        @pl.when(outer)
        def _():
            send(out_s.at[2, S_X], in_e.at[0], 1, "rs", 1, "ge", xn(1))
            send(out_s.at[2, S_Y], in_e.at[1], 1, "rs", 1, "ge", yn(1))

        @pl.when(inner)
        def _():
            send(out_s.at[2, S_X], in_z.at[1, 1], 1, "rs", 1, "g2xy", peer(2, 1))
            send(out_s.at[2, S_Y], in_z.at[1, 2], 1, "rs", 1, "g2xy", peer(2, 1))

        fill_sides(1)
        send(out_s.at[1, S_X], in_z.at[0, 1], 1, "rs", 1, "g1xy", peer(1, 1))
        send(out_s.at[1, S_Y], in_z.at[0, 2], 1, "rs", 1, "g1xy", peer(1, 1))

    gx_ref[...] = dot_nt(embed_grad, weight).astype(BF)

    @pl.when(lead)
    def _():
        arrived(in_xy, 1, "gxy3")
        put(
            3, S_O, FULL,
            base(3, "o", FULL) + in_xy[0].astype(F32) + in_xy[1].astype(F32),
        )
        send(out_s.at[3, S_O], in_z.at[gs_slot, 0], 1, "rs", 1, gs_key, peer(3, 1))

        @pl.when(outer)
        def _():
            arrived(in_e, 1, "ge")
            put(
                2, S_O, FULL,
                base(2, "o", FULL) + in_e[0].astype(F32) + in_e[1].astype(F32),
            )
            send(out_s.at[2, S_O], in_z.at[gs_slot, 0], 1, "rs", 1, gs_key, peer(2, 1))


    text_grad = jnp.dot(
        pair_grad(own_text, mine, t, bias, True), mine, preferred_element_type=F32
    )

    @pl.when(lead)
    def _():
        sides(0)
        arrived(in_z.at[0, pl.ds(1, 2)], 1, "g1xy")


        @pl.when(outer)
        def _():
            for cut in (A, B):
                put(0, S_X, cut, x_sum(0, cut) + in_z[0, 1, :, :, cut].astype(F32))
                put(0, S_Y, cut, y_sum(0, cut) + in_z[0, 2, :, :, cut].astype(F32))

        @pl.when(inner)
        def _():
            arrived(in_z.at[1, pl.ds(1, 2)], 1, "g2xy")
            for cut in (A, B):
                for r, fill in ((1, x_sum), (2, y_sum)):
                    put(
                        0, r, cut,
                        fill(0, cut) + in_z[0, r, :, :, cut].astype(F32)
                        + in_z[1, r, :, :, cut].astype(F32),
                    )

        for c in range(2):
            send(out_s.at[0, S_X, c], in_fin.at[0], 1, "rs", c, "fin", xn(c))
            send(out_s.at[0, S_Y, c], in_fin.at[1], 1, "rs", c, "fin", yn(c))

    text_grad = window(own_text, iw, text_grad)
    text_unit = t_ref[...].astype(F32) / text_length
    along = jnp.sum(text_unit * text_grad, axis=1, keepdims=True)
    gt_ref[...] = ((text_grad - text_unit * along) / text_length).astype(BF)

    @pl.when(lead)
    def _():
        total = base(0, "o", FULL)
        for i, key in enumerate(("g1o", "g2o", "g3o")):
            arrived(in_z.at[i, 0], 1, key)
            total += in_z[i, 0].astype(F32)
        pre_out[...] = total[0]
        send(pre_out, pre_in, 1, "pre", 0, "pre", partner)
        pre_in[...] = total[1]
        arrived(in_fin, 1, "fin")

    @pl.when(hub)
    def _():
        arrived(pre_in, 0, "pre")
        arrived(in_fin, 0, "fin")

    gw_ref[...] = pre_in[...] + in_fin[0].astype(F32) + in_fin[1].astype(F32)

    tw.drain()
    iw.drain()

    @pl.when(hub)
    def _():
        drained(shards(6), 0, "ag")
        drained(shards(n), 0, "g0")

    @pl.when(lead)
    def _():
        drained(shards(25), 1, "ag")
        drained(shards(n - 1), 1, "w")
        drained(shards(30), 1, "rs")
        drained(pre_out, 1, "pre")

    assert max(map(len, sends)) <= SENDS
    assert max(map(len, recvs)) <= RECVS


def fused(n, axis, image_features, head_weight, text_embeds, factor, bias):
    rows, width = image_features.shape
    own_rows, cols = head_weight.shape
    hbm = pl.BlockSpec(memory_space=pltpu.HBM)
    vmem = pl.BlockSpec(memory_space=pltpu.VMEM)
    two = (2, own_rows, cols)
    scratch = [
        ((rows, width), BF),
        ((rows, cols), BF),
        ((n, own_rows, cols), BF),
        ((rows, cols), BF),
        ((5, rows, cols), BF),
        ((rows, cols), BF),
        ((5, rows, cols), BF),
        ((width, rows), BF),
        ((4, 4) + two, F32),
        ((4, 4) + two, BF),
        ((4, 4) + two, BF),
        ((4, 4) + two, BF),
        ((4,) + two, BF),
        ((2,) + two, BF),
        ((3, 3) + two, BF),
        ((2,) + two, BF),
        (two, BF),
        ((own_rows, cols), F32),
        ((own_rows, cols), F32),
        ((rows, cols), F32),
    ]
    shapes = (((rows, width), BF), ((rows, cols), BF), ((own_rows, cols), F32))
    results = pl.pallas_call(
        functools.partial(kernel, n, axis),
        out_shape=tuple(pltpu.VMEM(s, d) for s, d in shapes),
        in_specs=[hbm] * 3 + [pl.BlockSpec(memory_space=pltpu.SMEM)],
        out_specs=(vmem, vmem, vmem),
        scratch_shapes=[pltpu.VMEM(s, d) for s, d in scratch]
        + [pltpu.SemaphoreType.DMA((k,)) for k in (5, SENDS, RECVS)]
        + [pltpu.SemaphoreType.REGULAR],
        compiler_params=pltpu.CompilerParams(
            collective_id=0, has_side_effects=True, vmem_limit_bytes=65413120
        ),
    )(image_features, head_weight, text_embeds, jnp.concatenate([factor, bias]))
    return pl.pallas_call(
        write_out,
        out_shape=tuple(jax.ShapeDtypeStruct(s, d) for s, d in shapes),
        in_specs=[vmem] * 3,
        out_specs=(hbm,) * 3,
        scratch_shapes=[pltpu.SemaphoreType.DMA((3,))],
        compiler_params=pltpu.CompilerParams(vmem_limit_bytes=2**20),
    )(*results)


def write_out(gx, gt, gw, gx_out, gt_out, gw_out, sems):
    pairs = ((gx, gx_out), (gt, gt_out), (gw, gw_out))
    copies = [pltpu.make_async_copy(a, b, sems.at[i]) for i, (a, b) in enumerate(pairs)]
    for c in copies:
        c.start()
    for c in copies:
        c.wait()


def passed_along(block, axis, distance):
    devices = range(lax.axis_size(axis))
    route = [((i - distance) % len(devices), i) for i in devices]
    return lax.ppermute(block, axis, route)


def normalize(rows):
    squares = jnp.sum(rows * rows, axis=1, keepdims=True)
    length = jnp.sqrt(squares + epsilon)
    return (rows / length, length)


def similarity_derivative(
    picture_sample_group,
    caption_sample_group,
    similarity_multiplier,
    neighbour_distance,
    outer_dimension_size,
):
    similarity_matrix = (
        similarity_multiplier
        * lax.dot_general(
            picture_sample_group,
            caption_sample_group,
            (((1,), (1,)), ((), ())),
            preferred_element_type=jnp.float32,
        )
        + neighbour_distance
    )
    if outer_dimension_size:
        matched = lax.broadcasted_iota(
            jnp.int32, similarity_matrix.shape, 0
        ) == lax.broadcasted_iota(jnp.int32, similarity_matrix.shape, 1)
        match_polarity = jnp.where(matched, 1.0, -1.0).astype(jnp.float32)
    else:
        match_polarity = -jnp.ones(similarity_matrix.shape, jnp.float32)
    return (
        -similarity_multiplier
        * match_polarity
        * jax.nn.sigmoid(-match_polarity * similarity_matrix)
    ).astype(jnp.bfloat16)


def project_back(grad, unit_rows, length):
    return (grad - unit_rows * jnp.sum(unit_rows * grad, axis=1, keepdims=True)) / length


def by_collectives(image_features, head_weight, text_embeds, natural_exponent_factor, logit_bias):
    full_weight = lax.all_gather(head_weight, "blk", axis=0, tiled=True)
    embedded = jnp.dot(image_features, full_weight, preferred_element_type=jnp.float32)
    image_unit, image_length = normalize(embedded)
    picture_embedding_mapped = image_unit.astype(jnp.bfloat16)
    text_unit, text_length = normalize(text_embeds.astype(jnp.float32))
    text_low = text_unit.astype(jnp.bfloat16)
    similarity_multiplier = jnp.exp(natural_exponent_factor[0])
    neighbour_distance = logit_bias[0]
    image_grad = jnp.zeros(image_unit.shape, jnp.float32)
    current_neighbour_tile = text_low
    for partition_portion in range(S):
        mapping_matrix = similarity_derivative(
            picture_embedding_mapped,
            current_neighbour_tile,
            similarity_multiplier,
            neighbour_distance,
            partition_portion == 0,
        )
        image_grad = image_grad + jnp.dot(
            mapping_matrix, current_neighbour_tile, preferred_element_type=jnp.float32
        )
        if partition_portion + 1 < S:
            current_neighbour_tile = passed_along(current_neighbour_tile, "blk", -1)
    text_grad = jnp.zeros(text_unit.shape, jnp.float32)
    passing = picture_embedding_mapped
    for partition_portion in range(S):
        mapping_matrix = similarity_derivative(
            passing, text_low, similarity_multiplier, neighbour_distance, partition_portion == 0
        )
        text_grad = text_grad + lax.dot_general(
            mapping_matrix, passing, (((0,), (0,)), ((), ())), preferred_element_type=jnp.float32
        )
        if partition_portion + 1 < S:
            passing = passed_along(passing, "blk", 1)
    embed_grad = project_back(image_grad, image_unit, image_length).astype(jnp.bfloat16)
    grad_text = project_back(text_grad, text_unit, text_length).astype(jnp.bfloat16)
    grad_features = lax.dot_general(
        embed_grad, full_weight, (((1,), (1,)), ((), ())), preferred_element_type=jnp.float32
    ).astype(jnp.bfloat16)
    grad_weight = lax.psum_scatter(
        lax.dot_general(
            image_features, embed_grad, (((0,), (0,)), ((), ())), preferred_element_type=jnp.float32
        ),
        "blk",
        scatter_dimension=0,
        tiled=True,
    )
    return (grad_features, grad_text, grad_weight)


def on_device(image_features, head_weight, text_embeds, natural_exponent_factor, logit_bias):
    n = lax.axis_size("blk")
    whole_tiles = head_weight.shape[0] % 16 == 0 and n % 8 == 0 and n // 8 == 4
    run = functools.partial(fused, n, "blk") if whole_tiles else by_collectives
    return run(image_features, head_weight, text_embeds, natural_exponent_factor, logit_bias)


def solution(mesh):
    return jax.shard_map(
        on_device,
        mesh=mesh,
        in_specs=(P("blk", None), P("blk", None), P("blk", None), P(), P()),
        out_specs=(P("blk", None), P("blk", None), P("blk", None)),
        check_vma=False,
    )
```

time: 81.7 us -> 74.2 us (0.908)
  the two profiles are of different devices: /device:TPU:16 before, /device:TPU:7 now
where the time goes in v2:
time: 74.2 us; the launch traced here: 73.7 us
  Pallas kernels  71.2 us (96%)
  between operations  1.93 us (3%)
    pallas_call x1, Pallas kernels, fused(): pl.pallas_call(functools.partial(kernel, n, axis), out_shape=tuple((pltpu...  70 us

profile of v2, /device:TPU:7, one launch (start us, length us, event | category | flops | bytes accessed | tf_op | source)
XLA Modules:
  0.0 73.7 jit_solution(16848458065829665107)
XLA Ops:
  1.9 0.6 pad_maximum_fusion.scalars
  2.5 70.0 %shard_map.76 = (bf16[256,1536]{1,0:T(8,128)(2,1)S(1)}, bf16[256,1152]{1,0:T(8,128)(2,1)S(1)}, f32[48,1152]{1,0:T(8,128)S(1)}) custom-call(bf16[256,1536]{1,0:T(8,128)(2,1)} %x_hbm.1, bf16[48,1152]{1,0:T(8,128)(2,1)} %w_hbm.1, bf16[256,1152]{1,0:T(8,128)(2,1)} %t_hbm.1, f32[2]{0:T(128)} %pad_maximum_fusion.scalars), custom_call_target="tpu_custom_call" | custom-call | tf_op jit(solution)/shard_map/pallas_call | solution.py:653
  72.5 1.2 %shard_map.77 = (bf16[256,1536]{1,0:T(8,128)(2,1)}, bf16[256,1152]{1,0:T(8,128)(2,1)}, f32[48,1152]{1,0:T(8,128)}) custom-call(bf16[256,1536]{1,0:T(8,128)(2,1)S(1)} %get-tuple-element.6.gx, bf16[256,1152]{1,0:T(8,128)(2,1)S(1)} %get-tuple-element.7.gt, f32[48,1152]{1,0:T(8,128)S(1)} %get-tuple-element.8.gw), custom_call_target="tpu_custom_call" | custom-call | tf_op jit(solution)/shard_map/pallas_call | solution.py:665

commit v3 on v2

--- a/solution.py
+++ b/solution.py
@@ -42,11 +42,11 @@
 
 def kernel(
     n, axis,
-    x_hbm, w_hbm, t_hbm, scalars,
+    x_hbm, w_hbm, t_hbm, lf_hbm, bias_hbm,
     gx_ref, gt_ref, gw_ref,
     x_ref, t_ref, w_all, text_low, text_in, image_low, image_in, xt, gz, from_core, to_core,
     out_s, in_d, in_xy, in_z, in_e, in_fin, pre_out, pre_in, embedded_ref,
-    load_sem, send_sem, recv_sem, credit,
+    factor_ref, bias_ref, load_sem, send_sem, recv_sem, credit,
 ):
     rows, width = x_ref.shape
     own_rows, cols = w_all.shape[1:]
@@ -117,19 +117,12 @@
         pl.semaphore_signal(barrier, inc=1, device_id=(p,), device_id_type=MESH)
 
     pairs = [
-        (w_hbm, w_all.at[me]), (t_hbm, t_ref),
+        (w_hbm, w_all.at[me]), (t_hbm, t_ref), (lf_hbm, factor_ref), (bias_hbm, bias_ref),
         (x_hbm, x_ref),
     ]
     loads = [pltpu.make_async_copy(a, b, load_sem.at[i]) for i, (a, b) in enumerate(pairs)]
     for c in loads:
         c.start()
-    for c in loads[1:2]:
-        c.wait()
-    t = jnp.exp(jnp.full((1, 1), scalars[0], F32))
-    bias = scalars[1]
-    text = t_ref[...].astype(F32)
-    text_length = jnp.sqrt(jnp.sum(text * text, axis=1, keepdims=True) + epsilon)
-    text_low[...] = (text / text_length).astype(BF)
     loads[0].wait()
 
     pl.semaphore_wait(barrier, len(peers))
@@ -271,6 +264,22 @@
     def _():
         first_sends(0)
         send(own, own, 0, "ag", 1, "w0", partner)
+
+    @pl.when(lead)
+    def _():
+        first_sends(1)
+        send(own, own, 1, "w", 0, ("w", 0), partner)
+
+    for c in loads[1:4]:
+        c.wait()
+    t = jnp.exp(jnp.full((1, 1), factor_ref[0], F32))
+    bias = bias_ref[0]
+    text = t_ref[...].astype(F32)
+    text_length = jnp.sqrt(jnp.sum(text * text, axis=1, keepdims=True) + epsilon)
+    text_low[...] = (text / text_length).astype(BF)
+
+    @pl.when(hub)
+    def _():
         tw.start_low(0)
         tw.wait_own()
         tw.start_high(0)
@@ -278,13 +287,11 @@
             pl.semaphore_wait(credit, 1)
             tw.start_low(c)
             tw.start_high(c)
-        for c in range(CHUNKS):
-            tw.far(c)
-
-    @pl.when(lead)
-    def _():
-        first_sends(1)
-        send(own, own, 1, "w", 0, ("w", 0), partner)
+            tw.far(c - 1)
+        tw.far(CHUNKS - 1)
+
+    @pl.when(lead)
+    def _():
         tw.leaf_sends()
 
         side_x(0, "px0")
@@ -322,7 +329,7 @@
         swap(2, "y")
         diagonal(1)
 
-    loads[2].wait()
+    loads[4].wait()
     xt[...] = x_ref[...].T
 
     @pl.when(hub)
@@ -465,11 +472,39 @@
         v = base(p, "y", cut)
         return v + in_d[p, :, :, cut].astype(F32) if cut is B else v
 
-    def fill_sides(p):
-        sides(p)
-        for cut in (A, B):
-            put(p, S_X, cut, x_sum(p, cut))
-            put(p, S_Y, cut, y_sum(p, cut))
+    def put_sides(p, first):
+        cx, cy = (B, A) if first else (A, B)
+        put(p, S_X, cx, x_sum(p, cx))
+        put(p, S_Y, cy, y_sum(p, cy))
+
+    def send_sides(p, first, buf, i, key, tx, ty):
+        cx, cy = (B, A) if first else (A, B)
+        for r, cut, target in ((0, cx, tx), (1, cy, ty)):
+            dst = buf.at[r, :, :, cut] if i is None else buf.at[i, r + 1, :, :, cut]
+            send(out_s.at[p, S_X + r, :, :, cut], dst, 1, "rs", 1, key, target)
+
+    def sides_of(p, first):
+        if not first:
+            sides(p)
+        put_sides(p, first)
+        if p == 3:
+            send_sides(p, first, in_xy, None, "gxy3", xn(1), yn(1))
+        if p == 1:
+            send_sides(p, first, in_z, 0, "g1xy", peer(1, 1), peer(1, 1))
+        if p == 2:
+            @pl.when(outer)
+            def _():
+                send_sides(p, first, in_e, None, "ge", xn(1), yn(1))
+
+            @pl.when(inner)
+            def _():
+                send_sides(p, first, in_z, 1, "g2xy", peer(2, 1), peer(2, 1))
+
+    gx_ref[...] = dot_nt(embed_grad, weight).astype(BF)
+
+    text_grad = jnp.dot(
+        pair_grad(own_text, mine, t, bias, True), mine, preferred_element_type=F32
+    )
 
     @pl.when(lead)
     def _():
@@ -477,6 +512,7 @@
         open_plane(2)
         open_plane(1)
         rest(3)
+        sides_of(3, True)
         rest(2)
 
         @pl.when(inner)
@@ -484,12 +520,12 @@
             put(2, S_O, FULL, base(2, "o", FULL))
             send(out_s.at[2, S_O], in_z.at[gs_slot, 0], 1, "rs", 1, gs_key, peer(2, 1))
 
+        sides_of(2, True)
         rest(1)
         put(1, S_O, FULL, base(1, "o", FULL))
         send(out_s.at[1, S_O], in_z.at[0, 0], 1, "rs", 1, "g1o", peer(1, 1))
-        fill_sides(3)
-        send(out_s.at[3, S_X], in_xy.at[0], 1, "rs", 1, "gxy3", xn(1))
-        send(out_s.at[3, S_Y], in_xy.at[1], 1, "rs", 1, "gxy3", yn(1))
+        sides_of(1, True)
+        sides_of(3, False)
         release()
         open_plane(0)
         rest(0)
@@ -511,23 +547,8 @@
 
     @pl.when(lead)
     def _():
-        fill_sides(2)
-
-        @pl.when(outer)
-        def _():
-            send(out_s.at[2, S_X], in_e.at[0], 1, "rs", 1, "ge", xn(1))
-            send(out_s.at[2, S_Y], in_e.at[1], 1, "rs", 1, "ge", yn(1))
-
-        @pl.when(inner)
-        def _():
-            send(out_s.at[2, S_X], in_z.at[1, 1], 1, "rs", 1, "g2xy", peer(2, 1))
-            send(out_s.at[2, S_Y], in_z.at[1, 2], 1, "rs", 1, "g2xy", peer(2, 1))
-
-        fill_sides(1)
-        send(out_s.at[1, S_X], in_z.at[0, 1], 1, "rs", 1, "g1xy", peer(1, 1))
-        send(out_s.at[1, S_Y], in_z.at[0, 2], 1, "rs", 1, "g1xy", peer(1, 1))
-
-    gx_ref[...] = dot_nt(embed_grad, weight).astype(BF)
+        sides_of(2, False)
+        sides_of(1, False)
 
     @pl.when(lead)
     def _():
@@ -537,20 +558,6 @@
             base(3, "o", FULL) + in_xy[0].astype(F32) + in_xy[1].astype(F32),
         )
         send(out_s.at[3, S_O], in_z.at[gs_slot, 0], 1, "rs", 1, gs_key, peer(3, 1))
-
-        @pl.when(outer)
-        def _():
-            arrived(in_e, 1, "ge")
-            put(
-                2, S_O, FULL,
-                base(2, "o", FULL) + in_e[0].astype(F32) + in_e[1].astype(F32),
-            )
-            send(out_s.at[2, S_O], in_z.at[gs_slot, 0], 1, "rs", 1, gs_key, peer(2, 1))
-
-
-    text_grad = jnp.dot(
-        pair_grad(own_text, mine, t, bias, True), mine, preferred_element_type=F32
-    )
 
     @pl.when(lead)
     def _():
@@ -578,6 +585,15 @@
         for c in range(2):
             send(out_s.at[0, S_X, c], in_fin.at[0], 1, "rs", c, "fin", xn(c))
             send(out_s.at[0, S_Y, c], in_fin.at[1], 1, "rs", c, "fin", yn(c))
+
+        @pl.when(outer)
+        def _():
+            arrived(in_e, 1, "ge")
+            put(
+                2, S_O, FULL,
+                base(2, "o", FULL) + in_e[0].astype(F32) + in_e[1].astype(F32),
+            )
+            send(out_s.at[2, S_O], in_z.at[gs_slot, 0], 1, "rs", 1, gs_key, peer(2, 1))
 
     text_grad = window(own_text, iw, text_grad)
     text_unit = t_ref[...].astype(F32) / text_length
@@ -653,15 +669,16 @@
     results = pl.pallas_call(
         functools.partial(kernel, n, axis),
         out_shape=tuple(pltpu.VMEM(s, d) for s, d in shapes),
-        in_specs=[hbm] * 3 + [pl.BlockSpec(memory_space=pltpu.SMEM)],
+        in_specs=[hbm] * 5,
         out_specs=(vmem, vmem, vmem),
         scratch_shapes=[pltpu.VMEM(s, d) for s, d in scratch]
+        + [pltpu.SMEM((1,), F32)] * 2
         + [pltpu.SemaphoreType.DMA((k,)) for k in (5, SENDS, RECVS)]
         + [pltpu.SemaphoreType.REGULAR],
         compiler_params=pltpu.CompilerParams(
             collective_id=0, has_side_effects=True, vmem_limit_bytes=65413120
         ),
-    )(image_features, head_weight, text_embeds, jnp.concatenate([factor, bias]))
+    )(image_features, head_weight, text_embeds, factor, bias)
     return pl.pallas_call(
         write_out,
         out_shape=tuple(jax.ShapeDtypeStruct(s, d) for s, d in shapes),

time: 74.2 us -> 72.8 us (0.981)
  no operation moved by 1% of the time
where the time goes in v3:
time: 72.8 us; the launch traced here: 72.5 us
  Pallas kernels  70.5 us (97%)
  between operations  1.93 us (3%)
    pallas_call x1, Pallas kernels, fused(): pl.pallas_call(functools.partial(kernel, n, axis), out_shape=tuple((pltpu...  69.4 us

profile of v3, /device:TPU:7, one launch (start us, length us, event | category | flops | bytes accessed | tf_op | source)
XLA Modules:
  0.0 72.5 jit_solution(17445970524235915236)
XLA Ops:
  1.9 69.4 %shard_map.76 = (bf16[256,1536]{1,0:T(8,128)(2,1)S(1)}, bf16[256,1152]{1,0:T(8,128)(2,1)S(1)}, f32[48,1152]{1,0:T(8,128)S(1)}) custom-call(bf16[256,1536]{1,0:T(8,128)(2,1)} %x_hbm.1, bf16[48,1152]{1,0:T(8,128)(2,1)} %w_hbm.1, bf16[256,1152]{1,0:T(8,128)(2,1)} %t_hbm.1, f32[1]{0:T(128)S(6)} %copy.8.lf_hbm, f32[1]{0:T(128)S(6)} %copy.9.bias_hbm), custom_call_target="tpu_custom_call" | custom-call | tf_op jit(solution)/shard_map/pallas_call | solution.py:669
  71.3 1.2 %shard_map.77 = (bf16[256,1536]{1,0:T(8,128)(2,1)}, bf16[256,1152]{1,0:T(8,128)(2,1)}, f32[48,1152]{1,0:T(8,128)}) custom-call(bf16[256,1536]{1,0:T(8,128)(2,1)S(1)} %get-tuple-element.6.gx, bf16[256,1152]{1,0:T(8,128)(2,1)S(1)} %get-tuple-element.7.gt, f32[48,1152]{1,0:T(8,128)S(1)} %get-tuple-element.8.gw), custom_call_target="tpu_custom_call" | custom-call | tf_op jit(solution)/shard_map/pallas_call | solution.py:682

commit v4 on v3

--- a/solution.py
+++ b/solution.py
@@ -283,12 +283,19 @@
         tw.start_low(0)
         tw.wait_own()
         tw.start_high(0)
-        for c in range(1, CHUNKS):
-            pl.semaphore_wait(credit, 1)
-            tw.start_low(c)
-            tw.start_high(c)
-            tw.far(c - 1)
-        tw.far(CHUNKS - 1)
+        pl.semaphore_wait(credit, 1)
+        tw.start_low(1)
+        tw.start_high(1)
+        tw.far(0)
+        pl.semaphore_wait(credit, 1)
+        tw.start_low(2)
+        tw.start_high(2)
+        tw.far(1)
+        pl.semaphore_wait(credit, 1)
+        tw.start_low(3)
+        tw.start_high(3)
+        tw.far(2)
+        tw.far(3)
 
     @pl.when(lead)
     def _():
@@ -380,8 +387,8 @@
     @pl.when(hub)
     def _():
         iw.hub_own()
-        for c in range(3):
-            iw.start_high(c)
+        iw.start_high(0)
+        iw.start_high(1)
 
     @pl.when(lead)
     def _():
@@ -395,8 +402,10 @@
     @pl.when(hub)
     def _():
         iw.wait_own()
-        for c in range(3):
-            iw.start_low(c)
+        iw.start_low(0)
+        iw.start_low(1)
+        iw.start_low(2)
+        iw.start_low(3)
 
     def window(low, win, grads):
         for i, q in enumerate((win.third(), 1, 0)):
@@ -532,14 +541,13 @@
 
     @pl.when(hub)
     def _():
-        for c in range(3):
-            iw.far(c)
-        for c in range(3, CHUNKS):
-            pl.semaphore_wait(credit, 1)
-            iw.start_low(c)
-            iw.start_high(c)
-        for c in range(3, CHUNKS):
-            iw.far(c)
+        iw.far(0)
+        iw.far(1)
+        iw.far(2)
+        pl.semaphore_wait(credit, 1)
+        iw.start_high(2)
+        iw.start_high(3)
+        iw.far(3)
         for c in range(CHUNKS):
             iw.near(1, c)
         for c in range(CHUNKS):

time: 72.8 us -> 72.2 us (level)
  no operation moved by 1% of the time
where the time goes in v4:
time: 72.2 us; the launch traced here: 72 us
  Pallas kernels  70.1 us (97%)
  between operations  1.93 us (3%)
    pallas_call x1, Pallas kernels, fused(): pl.pallas_call(functools.partial(kernel, n, axis), out_shape=tuple((pltpu...  68.9 us

profile of v4, /device:TPU:7, one launch (start us, length us, event | category | flops | bytes accessed | tf_op | source)
XLA Modules:
  0.0 72.0 jit_solution(10455458039295327897)
XLA Ops:
  1.9 68.9 %shard_map.76 = (bf16[256,1536]{1,0:T(8,128)(2,1)S(1)}, bf16[256,1152]{1,0:T(8,128)(2,1)S(1)}, f32[48,1152]{1,0:T(8,128)S(1)}) custom-call(bf16[256,1536]{1,0:T(8,128)(2,1)} %x_hbm.1, bf16[48,1152]{1,0:T(8,128)(2,1)} %w_hbm.1, bf16[256,1152]{1,0:T(8,128)(2,1)} %t_hbm.1, f32[1]{0:T(128)S(6)} %copy.8.lf_hbm, f32[1]{0:T(128)S(6)} %copy.9.bias_hbm), custom_call_target="tpu_custom_call" | custom-call | tf_op jit(solution)/shard_map/pallas_call | solution.py:677
  70.8 1.2 %shard_map.77 = (bf16[256,1536]{1,0:T(8,128)(2,1)}, bf16[256,1152]{1,0:T(8,128)(2,1)}, f32[48,1152]{1,0:T(8,128)}) custom-call(bf16[256,1536]{1,0:T(8,128)(2,1)S(1)} %get-tuple-element.6.gx, bf16[256,1152]{1,0:T(8,128)(2,1)S(1)} %get-tuple-element.7.gt, f32[48,1152]{1,0:T(8,128)S(1)} %get-tuple-element.8.gw), custom_call_target="tpu_custom_call" | custom-call | tf_op jit(solution)/shard_map/pallas_call | solution.py:690

commit v5 on v4

--- a/solution.py
+++ b/solution.py
@@ -30,8 +30,8 @@
 
 
 CHUNKS = 4
-SENDS = 16
-RECVS = 48
+SENDS = 6
+RECVS = 42
 
 
 class Keys(dict):
@@ -281,20 +281,20 @@
     @pl.when(hub)
     def _():
         tw.start_low(0)
+        tw.start_low(1)
         tw.wait_own()
         tw.start_high(0)
         pl.semaphore_wait(credit, 1)
-        tw.start_low(1)
-        tw.start_high(1)
+        tw.start_low(2)
+        tw.start_low(3)
         tw.far(0)
         pl.semaphore_wait(credit, 1)
-        tw.start_low(2)
+        tw.start_high(1)
+        tw.far(1)
+        tw.far(2)
+        pl.semaphore_wait(credit, 1)
         tw.start_high(2)
-        tw.far(1)
-        pl.semaphore_wait(credit, 1)
-        tw.start_low(3)
         tw.start_high(3)
-        tw.far(2)
         tw.far(3)
 
     @pl.when(lead)
@@ -309,6 +309,7 @@
         onto(0, "y", FULL, ("zy", 1), peer(1, 1))
         onto(0, "y", FULL, ("zy", 2), peer(2, 1), "ag", inner)
         swap(0, "y")
+        release()
         arrived(pair(3, "o"), 1, "o3")
         onto(3, "o", FULL, "px3", xn(1))
         onto(3, "o", FULL, "py3", yn(1))
@@ -329,7 +330,6 @@
         swap(3, "x")
         side_y(3, "py3")
         swap(3, "y")
-        release()
         side_x(2, ("zx", 2))
         swap(2, "x")
         side_y(2, ("zy", 2))

time: 72.2 us -> 72 us (level)
  no operation moved by 1% of the time
where the time goes in v5:
time: 72 us; the launch traced here: 71.9 us
  Pallas kernels  69.9 us (97%)
  between operations  1.93 us (3%)
    pallas_call x1, Pallas kernels, fused(): pl.pallas_call(functools.partial(kernel, n, axis), out_shape=tuple((pltpu...  68.8 us

profile of v5, /device:TPU:7, one launch (start us, length us, event | category | flops | bytes accessed | tf_op | source)
XLA Modules:
  0.0 71.9 jit_solution(9079076370841831879)
XLA Ops:
  1.9 68.8 %shard_map.76 = (bf16[256,1536]{1,0:T(8,128)(2,1)S(1)}, bf16[256,1152]{1,0:T(8,128)(2,1)S(1)}, f32[48,1152]{1,0:T(8,128)S(1)}) custom-call(bf16[256,1536]{1,0:T(8,128)(2,1)} %x_hbm.1, bf16[48,1152]{1,0:T(8,128)(2,1)} %w_hbm.1, bf16[256,1152]{1,0:T(8,128)(2,1)} %t_hbm.1, f32[1]{0:T(128)S(6)} %copy.8.lf_hbm, f32[1]{0:T(128)S(6)} %copy.9.bias_hbm), custom_call_target="tpu_custom_call" | custom-call | tf_op jit(solution)/shard_map/pallas_call | solution.py:677
  70.7 1.2 %shard_map.77 = (bf16[256,1536]{1,0:T(8,128)(2,1)}, bf16[256,1152]{1,0:T(8,128)(2,1)}, f32[48,1152]{1,0:T(8,128)}) custom-call(bf16[256,1536]{1,0:T(8,128)(2,1)S(1)} %get-tuple-element.6.gx, bf16[256,1152]{1,0:T(8,128)(2,1)S(1)} %get-tuple-element.7.gt, f32[48,1152]{1,0:T(8,128)S(1)} %get-tuple-element.8.gw), custom_call_target="tpu_custom_call" | custom-call | tf_op jit(solution)/shard_map/pallas_call | solution.py:690
